TPU v7x, 32 devices: a whole 2x2x4 slice. The times are simulated.
32 devices in a mesh: wide: 8 (over y, x, core), narrow: 4 (over z).
Axes of the slice: x: 2, y: 2, z: 4, core: 2. Of those that a mesh axis runs over, the one named last changes fastest.
Arguments:
- tokens: bfloat16 [65536, 768], P(('wide', 'narrow')), may hold values from -6 to 6
- cotangent: bfloat16 [65536, 768], P(('wide', 'narrow')), may hold values from -6 to 6
- segment_ids: int32 [128, 512], P(('wide', 'narrow')), may hold values from 0 to 3, never falling along the last dimension, each value on 1 to 256 neighbouring positions
- feature_ids: int32 [128, 512], P(('wide', 'narrow')), may hold values from 0 to 15
- attention_master: float32 [3072, 768], P(('wide', 'narrow')), may hold values from -1.1547005 to 1.1547005
- attention_first: float32 [3072, 768], P(('wide', 'narrow')), may hold values from -1024 to 1024
- attention_second: float32 [3072, 768], P(('wide', 'narrow')), may hold values from 327.68 to 262144
- feedforward_master: float32 [6144, 768], P(('wide', 'narrow')), may hold values from -0.14433757 to 0.14433757
- feedforward_first: float32 [6144, 768], P(('wide', 'narrow')), may hold values from -1024 to 1024
- feedforward_second: float32 [6144, 768], P(('wide', 'narrow')), may hold values from 327.68 to 262144
- vector_master: float32 [13, 768], P(None, ('wide', 'narrow')), may hold values from -0.8 to 1.5
- vector_first: float32 [13, 768], P(None, ('wide', 'narrow')), may hold values from -1024 to 1024
- vector_second: float32 [13, 768], P(None, ('wide', 'narrow')), may hold values from 327.68 to 262144
Outputs:
- block_out: bfloat16 [65536, 768], P(('wide', 'narrow'))
- tokens_grad: bfloat16 [65536, 768], P(('wide', 'narrow'))
- attention_master_new: float32 [3072, 768], P(('wide', 'narrow'))
- attention_first_new: float32 [3072, 768], P(('wide', 'narrow'))
- attention_second_new: float32 [3072, 768], P(('wide', 'narrow'))
- attention_copy: bfloat16 [3072, 768], P(('wide', 'narrow'))
- feedforward_master_new: float32 [6144, 768], P(('wide', 'narrow'))
- feedforward_first_new: float32 [6144, 768], P(('wide', 'narrow'))
- feedforward_second_new: float32 [6144, 768], P(('wide', 'narrow'))
- feedforward_copy: bfloat16 [6144, 768], P(('wide', 'narrow'))
- vector_master_new: float32 [13, 768], P(None, ('wide', 'narrow'))
- vector_first_new: float32 [13, 768], P(None, ('wide', 'narrow'))
- vector_second_new: float32 [13, 768], P(None, ('wide', 'narrow'))
- vector_copy: bfloat16 [13, 768], P(None, ('wide', 'narrow'))
All inputs are finite; a program needn't handle non-finite values.
Results may differ from a plain program's by a relative error of at most 0.015.
The roundings to bfloat16 on the way count: a program that leaves them out, or rounds other values in their place, can miss the bound.
Values may be sent and summed in bfloat16 or wider, within the bound.
A program may use at most 256 MiB of HBM per device.

v0:
```python
from functools import partial
import jax, jax.numpy as jnp
from jax import lax
from jax.experimental import pallas as pl
from jax.experimental.pallas import tpu as pltpu
from jax.sharding import PartitionSpec as P

D = 768
FF = 3072
HEADS = 12
HEAD_DIM = 64
NORM_EPS = 1e-05
AWAY = -1e30
F32, BF16 = jnp.float32, jnp.bfloat16
ERFC = (0.11841221385764535, 0.11979147087435008, 0.09737185909338779, 0.13434283549706147,
        -0.0652102059595758, 0.2202795624136942, -0.16009561537425632, 0.035107795064101)
VMEM = pltpu.VMEM


def nn(a, b):
    return lax.dot_general(a, b, (((1,), (0,)), ((), ())), preferred_element_type=F32)

def nt(a, b):
    return lax.dot_general(a, b, (((1,), (1,)), ((), ())), preferred_element_type=F32)

def tn(a, b):
    return lax.dot_general(a, b, (((0,), (0,)), ((), ())), preferred_element_type=F32)

def whole(shape):
    return pl.BlockSpec(shape, lambda *_: (0,) * len(shape), pipeline_mode=pl.Buffered(1))

def gelu_pair(h):
    size = jnp.abs(h)
    t = 1.0 / (1.0 + (0.42 * 0.7071067811865476) * size)
    bell = jnp.exp(h * h * -0.5)
    poly = jnp.full_like(t, ERFC[-1])
    for coef in ERFC[-2::-1]:
        poly = poly * t + coef
    tail = poly * t * bell
    below = jnp.where(h < 0, tail, 1.0 - tail)
    return h * below, below + h * bell * 0.3989422804014327

def column_of(row):
    return jnp.transpose(jnp.broadcast_to(row, (8, row.shape[1])))[:, :1]

def group_of(seg, feat):
    both = seg * 16 + feat
    return column_of(both) == both

def cost(gigaflops, megabytes):
    return pl.CostEstimate(flops=int(gigaflops * 1e9), bytes_accessed=int(megabytes * 1e6), transcendentals=0)


def fetch_weights(me, offsets, pieces, w_ref, sem):
    rows = pieces[0].shape[1]
    half = D // 2
    copies = []
    for j, offset in enumerate(offsets):
        for side in range(2):
            for col in range(2):
                owner = (me ^ offset[col]) if side == 0 else (me ^ offset[col] ^ offset[2])
                at = pl.ds(pl.multiple_of(owner * rows, 8), rows)
                copies.append(pltpu.make_async_copy(pieces[2 * side + col].at[j], w_ref.at[at, pl.ds(col * half, half)], sem))
    for c in copies:
        c.start()
    for c in copies:
        c.wait()

def attend_forward(i, tok_ref, seg_ref, feat_ref, w_ref, vec_ref, mixed_ref, q_ref, k_ref, v_ref, ctx_ref, lse_ref, bias_scr, service):
    seg = seg_ref[pl.ds(i, 1), :]
    feat = feat_ref[pl.ds(i, 1), :]
    length = seg.shape[1]
    bias_scr[...] = jnp.where(column_of(seg) == seg, 0.0, AWAY)
    group = group_of(seg, feat)
    members = jnp.sum(group.astype(F32), axis=1, keepdims=True)
    tok = tok_ref[...]
    merging = nn(group.astype(F32).astype(BF16), tok) / members
    mixed = tok.astype(F32) + vec_ref[0:1, :] * merging
    mixed_ref[...] = mixed
    mb = mixed.astype(BF16)
    ctx_ref[0] = mb
    q_ref[...] = ((nn(mb, w_ref[0:D, :]) + vec_ref[1:2, :]) * 0.125).astype(BF16)
    k_ref[...] = nn(mb, w_ref[D:2 * D, :]).astype(BF16)
    v_ref[...] = (nn(mb, w_ref[2 * D:3 * D, :]) + vec_ref[2:3, :]).astype(BF16)
    lane = lax.broadcasted_iota(jnp.int32, (length, 128), 1)
    low = lane < HEAD_DIM
    lse_ref[...] = jnp.zeros_like(lse_ref)

    def pair(p, carry):
        at = pl.ds(pl.multiple_of(p * 128, 128), 128)
        qp = q_ref[:, at]
        kp = k_ref[:, at]
        vp = v_ref[:, at]
        outs = []
        zero = jnp.zeros_like(qp)
        for half in range(2):
            mine = low if half == 0 else jnp.logical_not(low)
            s = nt(jnp.where(mine, qp, zero), kp) + bias_scr[...]
            top = jnp.max(s, axis=1, keepdims=True)
            e = jnp.exp(s - top)
            total = jnp.sum(e, axis=1, keepdims=True)
            o = nn(e.astype(BF16), vp) * (1.0 / total)
            outs.append(o)
            lse_ref[...] = jnp.where(lane == 2 * p + half, top + jnp.log(total), lse_ref[...])
        ctx_ref[1, :, at] = jnp.where(low, outs[0], outs[1]).astype(BF16)
        return carry
    service(0)
    lax.fori_loop(0, HEADS // 4, pair, 0)
    service(1)
    lax.fori_loop(HEADS // 4, HEADS // 2, pair, 0)
    service(2)


def k1_body(first_seq, offsets, kept, self_ref, tok_ref, seg_ref, feat_ref, vec_ref, *rest):
    if kept:
        w_ref, rest = rest[0], rest[1 + kept:]
        mixed_ref, q_ref, k_ref, v_ref, ctx_ref, lse_ref, bias_scr = rest
    else:
        pieces, rest = rest[:4], rest[4:]
        mixed_ref, q_ref, k_ref, v_ref, ctx_ref, lse_ref, w_ref, bias_scr, sem = rest
    i = pl.program_id(0) + first_seq

    if not kept:
        @pl.when(pl.program_id(0) == 0)
        def _():
            fetch_weights(self_ref[0], offsets, pieces, w_ref, sem)

    attend_forward(i, tok_ref, seg_ref, feat_ref, w_ref, vec_ref, mixed_ref, q_ref, k_ref, v_ref, ctx_ref, lse_ref, bias_scr, lambda point: None)


def k1(first_seq, count, me, tokens, seg, feat, weights, offsets, vec, kept):
    seqs, length = seg.shape
    blk = pl.BlockSpec((length, D), lambda i, s: (i + first_seq, 0))
    both = pl.BlockSpec((2, length, D), lambda i, s: (0, i + first_seq, 0))
    narrow = pl.BlockSpec((length, 128), lambda i, s: (i + first_seq, 0))
    n = seqs * length
    o = lambda dt: jax.ShapeDtypeStruct((n, D), dt)
    any_spec = pl.BlockSpec(memory_space=pl.ANY)
    out_specs = [blk] * 4 + [both, narrow]
    out_shape = [o(F32), o(BF16), o(BF16), o(BF16), jax.ShapeDtypeStruct((2, n, D), BF16), jax.ShapeDtypeStruct((n, 128), F32)]
    scratch = [VMEM((length, length), F32)]
    if kept:
        weight_specs = [pl.BlockSpec((3 * D, D), lambda i, s: (0, 0), pipeline_mode=pl.Buffered(1))]
    else:
        weight_specs = [any_spec] * 4
        out_specs = out_specs + [whole((4 * D, D))]
        out_shape = out_shape + [jax.ShapeDtypeStruct((4 * D, D), BF16)]
        scratch = scratch + [pltpu.SemaphoreType.DMA]
    return pl.pallas_call(
        partial(k1_body, first_seq, offsets, len(kept)),
        grid_spec=pltpu.PrefetchScalarGridSpec(
            num_scalar_prefetch=1, grid=(count,),
            in_specs=[blk, whole(seg.shape), whole(feat.shape), whole(vec.shape)] + weight_specs + [any_spec] * len(kept),
            out_specs=out_specs, scratch_shapes=scratch,
        ),
        out_shape=out_shape,
        input_output_aliases={6 + j: j for j in range(len(kept))},
        cost_estimate=cost(count * 11, count * 4),
        name="mix_attend",
    )(me, tokens, seg, feat, vec, *weights, *kept)

MESH = pl.DeviceIdType.MESH


def flips(x, mask):
    bit = 1
    while bit <= mask:
        if mask & bit:
            x = x + bit - 2 * bit * ((x // bit) % 2)
        bit *= 2
    return x


class Spreading:
    def __init__(self, wide, narrow, shard, full, columns, sems):
        self.narrow, self.masks = narrow, wide // 2
        self.bits = [1 << b for b in range((wide // 2).bit_length() - 1)]
        w, self.z = lax.axis_index("wide"), lax.axis_index("narrow")
        self.o, self.c = w // 2, w % 2
        self.shard, self.full, self.columns = shard, full, columns
        self.line_out, self.line_in, self.tree_out, self.tree_in, self.core_out, self.core_in, self.own = sems

    def at(self, r, k, c=None, h=None):
        c = self.c if c is None else c
        rows = self.shard.shape[0]
        owner = (2 * flips(self.o, r) + c) * self.narrow + flips(self.z, k)
        where = pl.ds(pl.multiple_of(owner * rows, 8), rows)
        if h is None:
            return self.full.at[where, :]
        return self.full.at[where, pl.ds(*self.columns[h][:2])]

    def source(self, r, k, h=None):
        if r or k:
            return self.at(r, k, None, h)
        return self.shard if h is None else self.shard.at[:, pl.ds(*self.columns[h][:2])]

    def keep(self):
        return pltpu.make_async_copy(self.shard, self.at(0, 0), self.own)

    def line(self, k, arriving=False):
        return pltpu.make_async_remote_copy(
            self.shard, self.at(0, k if arriving else 0), self.line_out.at[k - 1], self.line_in.at[k - 1],
            device_id=(2 * self.o + self.c, flips(self.z, k)), device_id_type=MESH)

    def tree(self, r, k, h, bit, arriving=False):
        there = r if arriving else r ^ bit
        n = (k * len(self.columns) + h) * self.masks + there
        part = self.at(r, k, None, h)
        return pltpu.make_async_remote_copy(
            part if arriving else self.source(r, k, h), part, self.tree_out.at[n], self.tree_in.at[n],
            device_id=(2 * flips(self.o, bit) + self.c, self.z), device_id_type=MESH)

    def core(self, r, k, arriving=False):
        n = k * self.masks + r
        part = self.at(r, k, 1 - self.c if arriving else None)
        return pltpu.make_async_remote_copy(
            part if arriving else self.source(r, k), part, self.core_out.at[n], self.core_in.at[n],
            device_id=(2 * self.o + 1 - self.c, self.z), device_id_type=MESH)

    def onward(self, r, h):
        if self.columns[h][2]:
            return [b for b in reversed(self.bits) if r == 0 or b < (r & -r)]
        return [b for b in self.bits if b > r]

    def last_bit(self, r, h):
        if self.columns[h][2]:
            return r & -r
        return 1 << (r.bit_length() - 1)

    def open(self):
        self.keep().start()
        for k in range(1, self.narrow):
            self.line(k).start()

    def send_on(self, r, k, h):
        for bit in self.onward(r, h):
            self.tree(r, k, h, bit).start()

    def roots(self, k):
        if k:
            self.line(k, True).wait_recv()
        for h in range(len(self.columns)):
            self.send_on(0, k, h)
        self.core(0, k).start()

    def relay(self, r, k):
        for h in range(len(self.columns)):
            self.tree(r, k, h, self.last_bit(r, h), True).wait_recv()
            self.send_on(r, k, h)
        self.core(r, k).start()

    def close(self):
        for k in range(self.narrow):
            for r in range(self.masks):
                self.core(r, k, True).wait_recv()
        self.keep().wait()

    def drain(self):
        for k in range(self.narrow):
            if k:
                self.line(k).wait_send()
            for r in range(self.masks):
                for h in range(len(self.columns)):
                    for bit in self.onward(r, h):
                        self.tree(r, k, h, bit).wait_send()
                self.core(r, k).wait_send()


def spreading_sems(wide, narrow, halves):
    dma = pltpu.SemaphoreType.DMA
    tree, core = narrow * halves * (wide // 2), narrow * (wide // 2)
    return [dma((narrow - 1,)), dma((narrow - 1,)), dma((tree,)), dma((tree,)), dma((core,)), dma((core,)), dma]


def greet(wide, narrow):
    barrier = pltpu.get_barrier_semaphore()
    w, z = lax.axis_index("wide"), lax.axis_index("narrow")
    o, c = w // 2, w % 2
    peers = [(w, flips(z, k)) for k in range(1, narrow)] + [(2 * o + 1 - c, z)]
    bit = 1
    while bit < wide // 2:
        peers.append((2 * flips(o, bit) + c, z))
        bit *= 2
    for peer in peers:
        pl.semaphore_signal(barrier, inc=1, device_id=peer, device_id_type=MESH)
    pl.semaphore_wait(barrier, len(peers))


def gathering_k1_body(wide, narrow, cols, steps, tok_ref, seg_ref, feat_ref, att_ref, ff_ref, vs_ref,
                      mixed_ref, q_ref, k_ref, v_ref, ctx_ref, lse_ref, vec_ref, wout_ref, fout_ref,
                      bias_scr, w_ref, vs_scr, put_sem, *sems):
    i = pl.program_id(0)
    half = D // 2
    count = len(sems) // 3
    pairs = [(0, half, False), (half, half, True)]
    att = Spreading(wide, narrow, att_ref, w_ref, pairs, sems[:count])
    ff = Spreading(wide, narrow, ff_ref, fout_ref, pairs, sems[count:2 * count])
    vs = Spreading(wide, narrow, vs_ref, vs_scr, [(0, 128, False)], sems[2 * count:])
    singles = [r for r in range(1, wide // 2)]
    save = pltpu.make_async_copy(w_ref, wout_ref, put_sem)

    @pl.when(i == 0)
    def _():
        greet(wide, narrow)
        for one in (vs, att, ff):
            one.open()
        for k in range(narrow):
            vs.roots(k)
            att.roots(k)
        ff.roots(0)
        for r in singles:
            for k in range(narrow):
                vs.relay(r, k)
                att.relay(r, k)
        vs.close()
        vec = jnp.zeros((16, D), F32)
        row = lax.broadcasted_iota(jnp.int32, (128, D), 0)
        col = lax.broadcasted_iota(jnp.int32, (128, D), 1)
        for d in range(wide * narrow):
            pick = jnp.logical_and(row < cols, col == row + cols * d).astype(F32).astype(BF16)
            vec = vec + nn(vs_scr[16 * d:16 * d + 16, :], pick)
        vec_ref[...] = vec
        att.close()
        save.start()

    plan = [lambda k=k: ff.roots(k) for k in range(1, narrow)]
    for r in singles:
        plan += [lambda r=r, k=k: ff.relay(r, k) for k in range(narrow)]

    def service(point):
        for s in range(steps):
            todo = slots.get((s, point), ())
            if todo:
                @pl.when(i == s)
                def _(todo=todo):
                    for act in todo:
                        act()
    total = steps * 3 - 1
    slots = {}
    for n, act in enumerate(plan):
        spot = n * total // len(plan)
        slots.setdefault((spot // 3, spot % 3), []).append(act)

    attend_forward(i, tok_ref, seg_ref, feat_ref, w_ref, vec_ref, mixed_ref, q_ref, k_ref, v_ref, ctx_ref, lse_ref, bias_scr, service)

    @pl.when(i == steps - 1)
    def _():
        ff.close()
        for one in (vs, att, ff):
            one.drain()
        save.wait()


def gathering_k1(wide, narrow, tokens, seg, feat, att_shard, ff_shard, vec_shard):
    seqs, length = seg.shape
    n, devices = seqs * length, wide * narrow
    vs = jnp.pad(vec_shard, ((0, 16 - vec_shard.shape[0]), (0, 128 - vec_shard.shape[1])))
    blk = pl.BlockSpec((length, D), lambda i: (i, 0))
    any_spec = pl.BlockSpec(memory_space=pl.ANY)
    o = lambda dt: jax.ShapeDtypeStruct((n, D), dt)
    sems = spreading_sems(wide, narrow, 2) * 2 + spreading_sems(wide, narrow, 1)
    return pl.pallas_call(
        partial(gathering_k1_body, wide, narrow, vec_shard.shape[1], seqs), grid=(seqs,),
        in_specs=[blk, whole(seg.shape), whole(feat.shape), any_spec, any_spec, any_spec],
        out_specs=[blk] * 4 + [pl.BlockSpec((2, length, D), lambda i: (0, i, 0)), pl.BlockSpec((length, 128), lambda i: (i, 0)),
                               whole((16, D)), any_spec, any_spec],
        out_shape=[o(F32), o(BF16), o(BF16), o(BF16), jax.ShapeDtypeStruct((2, n, D), BF16), jax.ShapeDtypeStruct((n, 128), F32),
                   jax.ShapeDtypeStruct((16, D), F32), jax.ShapeDtypeStruct((4 * D, D), BF16), jax.ShapeDtypeStruct((2 * FF, D), BF16)],
        scratch_shapes=[VMEM((length, length), F32), VMEM((4 * D, D), BF16), VMEM((16 * devices, 128), BF16), pltpu.SemaphoreType.DMA, *sems],
        compiler_params=pltpu.CompilerParams(collective_id=0, has_side_effects=True),
        cost_estimate=cost(60, 60),
        name="gather_attend",
    )(tokens, seg, feat, att_shard, ff_shard, vs)

def norm_parts(z):
    mean = jnp.mean(z, axis=1, keepdims=True)
    c = z - mean
    var = jnp.mean(c * c, axis=1, keepdims=True)
    inv = lax.rsqrt(var + NORM_EPS)
    return c * inv, inv

def norm_pull(g, xhat, inv):
    a = jnp.mean(g, axis=1, keepdims=True)
    b = jnp.mean(g * xhat, axis=1, keepdims=True)
    return (g - a - xhat * b) * inv

def colsum(x):
    return jnp.sum(x, axis=0, keepdims=True)

def k2_body(offsets, self_ref, mixed_ref, ctx_ref, cot_ref, wo_ref, vec_ref, *rest):
    if offsets:
        pieces, rest = rest[:4], rest[4:]
        out_ref, first_ref, fb_ref, dctx_ref, wide_ref, slim_ref, vg_ref, gp_scr, sum_scr, wf_ref, sem = rest
    else:
        wf_ref, out_ref, first_ref, fb_ref, dctx_ref, wide_ref, slim_ref, vg_ref, gp_scr, sum_scr = rest
    ctx_ref = ctx_ref.at[0]
    hg_ref, act_ref = wide_ref.at[0], wide_ref.at[1]
    nb_ref, bg_ref = slim_ref.at[0], slim_ref.at[1]
    @pl.when(pl.program_id(0) == 0)
    def _():
        vg_ref[...] = jnp.zeros_like(vg_ref)
        if offsets:
            fetch_weights(self_ref[0], offsets, pieces, wf_ref, sem)

    ex = FF // D
    first_sum = mixed_ref[...] + nn(ctx_ref[...], wo_ref[...]) + vec_ref[3:4, :]
    xhat1, inv1 = norm_parts(first_sum)
    normed = xhat1 * vec_ref[4:5, :] + vec_ref[5:6, :]
    nb_ref[...] = normed.astype(BF16)
    sum_scr[...] = normed + vec_ref[6 + ex:7 + ex, :]
    for c in range(ex):
        at = pl.ds(c * D, D)
        h = nt(nb_ref[...], wf_ref[at, :]) + vec_ref[6 + c:7 + c, :]
        act, slope = gelu_pair(h)
        act_ref[:, at] = act.astype(BF16)
        gp_scr[:, at] = slope.astype(gp_scr.dtype)
        sum_scr[...] += nn(act_ref[:, at], wf_ref[pl.ds(FF + c * D, D), :])
    xhat2, inv2 = norm_parts(sum_scr[...])
    out_ref[...] = (xhat2 * vec_ref[7 + ex:8 + ex, :] + vec_ref[8 + ex:9 + ex, :]).astype(BF16)
    cot = cot_ref[...].astype(F32)
    vg_ref[4 + ex:5 + ex, :] += colsum(cot * xhat2)
    vg_ref[5 + ex:6 + ex, :] += colsum(cot)
    gs = norm_pull(cot * vec_ref[7 + ex:8 + ex, :], xhat2, inv2)
    vg_ref[3 + ex:4 + ex, :] += colsum(gs)
    bg_ref[...] = gs.astype(BF16)
    sum_scr[...] = gs
    for c in range(ex):
        at = pl.ds(c * D, D)
        hg = nt(bg_ref[...], wf_ref[pl.ds(FF + c * D, D), :]) * gp_scr[:, at].astype(F32)
        vg_ref[3 + c:4 + c, :] += colsum(hg)
        hg_ref[:, at] = hg.astype(BF16)
        sum_scr[...] += nn(hg_ref[:, at], wf_ref[at, :])
    ng = sum_scr[...]
    vg_ref[1:2, :] += colsum(ng * xhat1)
    vg_ref[2:3, :] += colsum(ng)
    fgr = norm_pull(ng * vec_ref[4:5, :], xhat1, inv1)
    vg_ref[0:1, :] += colsum(fgr)
    first_ref[...] = fgr
    fb_ref[...] = fgr.astype(BF16)
    dctx_ref[...] = nt(fb_ref[...], wo_ref[...]).astype(BF16)


def k2(me, mixed, ctx, cot, att, ff, offsets, vec, tile=256):
    n = mixed.shape[0]
    blk = pl.BlockSpec((tile, D), lambda i, s: (i, 0))
    o = lambda *w, dt=BF16: jax.ShapeDtypeStruct(w, dt)
    any_spec = pl.BlockSpec(memory_space=pl.ANY)
    return pl.pallas_call(
        partial(k2_body, offsets),
        grid_spec=pltpu.PrefetchScalarGridSpec(
            num_scalar_prefetch=1, grid=(n // tile,),
            in_specs=[blk, pl.BlockSpec((1, tile, D), lambda i, s: (1, i, 0)), blk,
                      pl.BlockSpec((D, D), lambda i, s: (3, 0), pipeline_mode=pl.Buffered(1)), whole(vec.shape)]
            + ([any_spec] * 4 if offsets else [whole(ff[0].shape)]),
            out_specs=[blk, blk, blk, blk, pl.BlockSpec((2, tile, FF), lambda i, s: (0, i, 0)),
                       pl.BlockSpec((2, tile, D), lambda i, s: (0, i, 0)), pl.BlockSpec((16, D), lambda i, s: (0, 0))],
            scratch_shapes=[VMEM((tile, FF), F32), VMEM((tile, D), F32)]
            + ([VMEM((2 * FF, D), BF16), pltpu.SemaphoreType.DMA] if offsets else []),
        ),
        out_shape=[o(n, D), o(n, D, dt=F32), o(n, D), o(n, D), o(2, n, FF), o(2, n, D), o(16, D, dt=F32)],
        cost_estimate=cost(60, 80),
        name="feed_forward",
    )(me, mixed, ctx, cot, att, vec, *ff)

def dw_body(rows, side_ref, lhs_ref, rhs_ref, out_ref):
    step = 128 if rows % 256 else 256

    def chunk(c, carry):
        at = pl.ds(pl.multiple_of(c * step, step), step)
        out_ref[0, at, :] = tn(lhs_ref[0, :, at], rhs_ref[0]).astype(BF16)
        return carry
    lax.fori_loop(0, rows // step, chunk, 0)


def dw(side, lhs, rhs, rows, count):
    n, span = lhs.shape[1:]
    per = span // rows
    repeats = rhs.shape[0] // lhs.shape[0]
    tall = lambda i, s: (2 * i + s[0]) // per
    left = (lambda t: t // 3) if repeats == 2 else (lambda t: t)
    return pl.pallas_call(
        partial(dw_body, rows),
        grid_spec=pltpu.PrefetchScalarGridSpec(
            num_scalar_prefetch=1, grid=(count,),
            in_specs=[pl.BlockSpec((1, n, rows), lambda i, s: (left(tall(i, s)), 0, (2 * i + s[0]) % per)),
                      pl.BlockSpec((1, n, D), lambda i, s: (tall(i, s), 0, 0))],
            out_specs=pl.BlockSpec((1, rows, D), lambda i, s: (i, 0, 0)),
        ),
        out_shape=jax.ShapeDtypeStruct((count, rows, D), BF16),
        cost_estimate=cost(2e-9 * n * rows * D * count, 10),
        name="weight_grad",
    )(side, lhs, rhs)

def k3_body(first_seq, kept, q_ref, k_ref, v_ref, ctx_ref, dctx_ref, fb_ref, lse_ref, seg_ref, *rest):
    d_ref, vg_ref, bias_scr, lse_scr, del_scr = rest[kept:]
    ctx_ref = ctx_ref.at[0]
    dq_ref, dk_ref, dv_ref = d_ref.at[0], d_ref.at[1], d_ref.at[2]
    d_ref[3] = fb_ref[...]
    i = pl.program_id(0) + first_seq

    @pl.when(pl.program_id(0) == 0)
    def _():
        vg_ref[...] = jnp.zeros_like(vg_ref)
    seg = seg_ref[pl.ds(i, 1), :]
    length = seg.shape[1]
    bias_scr[...] = jnp.where(column_of(seg) == seg, 0.0, AWAY)
    lse_scr[...] = jnp.transpose(lse_ref[...])[:16, :]
    prod = dctx_ref[...].astype(F32) * ctx_ref[...].astype(F32)
    pick = (lax.broadcasted_iota(jnp.int32, (16, D), 1) // HEAD_DIM == lax.broadcasted_iota(jnp.int32, (16, D), 0)).astype(F32)
    del_scr[...] = lax.dot_general(pick, prod, (((1,), (1,)), ((), ())), precision=lax.Precision.HIGHEST, preferred_element_type=F32)
    low = lax.broadcasted_iota(jnp.int32, (length, 128), 1) < HEAD_DIM

    def pair(p, carry):
        at = pl.ds(pl.multiple_of(p * 128, 128), 128)
        qp, kp, vp, op = q_ref[:, at], k_ref[:, at], v_ref[:, at], dctx_ref[:, at]
        zero = jnp.zeros_like(qp)
        got = []
        for half in range(2):
            mine = low if half == 0 else jnp.logical_not(low)
            st = nt(jnp.where(mine, kp, zero), qp) + bias_scr[...]
            pt = jnp.exp(st - lse_scr[pl.ds(2 * p + half, 1), :])
            dv = nn(pt.astype(BF16), op)
            dpt = nt(jnp.where(mine, vp, zero), op)
            dst = (pt * (dpt - del_scr[pl.ds(2 * p + half, 1), :])).astype(BF16)
            dk = nn(dst, qp)
            dq = tn(dst, kp)
            got.append((dq, dk, dv))
        dq, dk, dv = (jnp.where(low, a, b) for a, b in zip(*got))
        dqb = dq.astype(BF16) * jnp.bfloat16(0.125)
        dvb = dv.astype(BF16)
        dq_ref[:, at] = dqb
        dk_ref[:, at] = dk.astype(BF16)
        dv_ref[:, at] = dvb
        vg_ref[0:1, at] += colsum(dqb.astype(F32))
        vg_ref[1:2, at] += colsum(dvb.astype(F32))
        return carry
    lax.fori_loop(0, HEADS // 2, pair, 0)


def k3(first_seq, count, q, k, v, ctx, dctx, fb, lse, seg, kept):
    seqs, length = seg.shape
    n = seqs * length
    blk = pl.BlockSpec((length, D), lambda i: (i + first_seq, 0))
    return pl.pallas_call(
        partial(k3_body, first_seq, len(kept)), grid=(count,),
        in_specs=[blk] * 3 + [pl.BlockSpec((1, length, D), lambda i: (1, i + first_seq, 0)), blk, blk,
                              pl.BlockSpec((length, 128), lambda i: (i + first_seq, 0)), whole((seqs, length))]
        + [pl.BlockSpec(memory_space=pl.ANY)] * len(kept),
        out_specs=[pl.BlockSpec((4, length, D), lambda i: (0, i + first_seq, 0)), pl.BlockSpec((8, D), lambda i: (0, 0))],
        out_shape=[jax.ShapeDtypeStruct((4, n, D), BF16), jax.ShapeDtypeStruct((8, D), F32)],
        scratch_shapes=[VMEM((length, length), F32), VMEM((16, length), F32), VMEM((16, length), F32)],
        input_output_aliases={8 + j: j for j in range(len(kept))},
        cost_estimate=cost(count * 12, count * 6),
        name="attend_back",
    )(q, k, v, ctx, dctx, fb, lse, seg, *kept)

def k4_body(first_seq, kept, first_ref, d_ref, tok_ref, seg_ref, feat_ref, w_ref, vec_ref, *rest):
    tg_ref, vg_ref = rest[kept:]
    i = pl.program_id(0) + first_seq
    dq_ref, dk_ref, dv_ref = d_ref.at[0], d_ref.at[1], d_ref.at[2]

    @pl.when(pl.program_id(0) == 0)
    def _():
        vg_ref[...] = jnp.zeros_like(vg_ref)
    group = group_of(seg_ref[pl.ds(i, 1), :], feat_ref[pl.ds(i, 1), :])
    gf = group.astype(F32)
    members = jnp.sum(gf, axis=1, keepdims=True)
    gb = gf.astype(BF16)
    tok = tok_ref[...]
    merging = nn(gb, tok) / members
    mg = (first_ref[...] + nt(dq_ref[...], w_ref[0:D, :]) + nt(dk_ref[...], w_ref[D:2 * D, :])
          + nt(dv_ref[...], w_ref[2 * D:3 * D, :]))
    vg_ref[0:1, :] += colsum(mg * merging)
    spread = (vec_ref[0:1, :] * mg / members).astype(BF16)
    tg_ref[...] = (mg + nn(gb, spread)).astype(BF16)


def k4(first_seq, count, first, d, tokens, seg, feat, att, vec, kept):
    seqs, length = seg.shape
    n = seqs * length
    blk = pl.BlockSpec((length, D), lambda i: (i + first_seq, 0))
    return pl.pallas_call(
        partial(k4_body, first_seq, len(kept)), grid=(count,),
        in_specs=[blk, pl.BlockSpec((3, length, D), lambda i: (0, i + first_seq, 0)), blk, whole(seg.shape), whole(feat.shape),
                  pl.BlockSpec((3 * D, D), lambda i: (0, 0), pipeline_mode=pl.Buffered(1)), whole(vec.shape)]
        + [pl.BlockSpec(memory_space=pl.ANY)] * len(kept),
        out_specs=[blk, pl.BlockSpec((8, D), lambda i: (0, 0))],
        out_shape=[jax.ShapeDtypeStruct((n, D), BF16), jax.ShapeDtypeStruct((8, D), F32)],
        input_output_aliases={7 + j: j for j in range(len(kept))},
        cost_estimate=cost(count * 3, count * 5),
        name="token_grad",
    )(first, d, tokens, seg, feat, att, vec, *kept)

def adam_step(master, first, second, gradient, rate):
    first_new = BETA * first + (1.0 - BETA) * gradient
    second_new = BETA * second + (1.0 - BETA) * gradient * gradient
    correction = 1.0 - BETA**ADAM_STEP
    master_new = master - rate * (
        first_new / correction / (jnp.sqrt(second_new / correction) + ADAM_EPS) + DECAY * master
    )
    return (master_new, first_new, second_new)


BETA = 0.5
ADAM_STEP = 3
ADAM_EPS = 1e-08
DECAY = 0.01
VECTOR_RATE = 0.1
BOTH = ("wide", "narrow")


def rates(rows, split, first_rate, second_rate):
    index = (lax.axis_index(BOTH) * rows + jnp.arange(rows))[:, None]
    return jnp.where(index < split, first_rate, second_rate)


def tie(*groups):
    return lax.optimization_barrier(groups)


def bit_steps(wide, narrow):
    inner = [1 << b for b in range(narrow.bit_length() - 1)]
    outer = [narrow << b for b in range(1, wide.bit_length() - 1)]
    return inner, outer, narrow


def swap(value, bit, devices):
    return lax.ppermute(value, BOTH, [(i, i ^ bit) for i in range(devices)])


class Gather:
    def __init__(self, shard, wide, narrow):
        self.devices = wide * narrow
        inner, outer, self.core = bit_steps(wide, narrow)
        self.turns = [(bit,) for bit in reversed(inner)] + list(zip(outer, reversed(outer))) + [(self.core, self.core)]
        self.held, self.offsets, self.last = [shard[None]], [[0]], None

    def turn(self):
        bits = self.turns.pop(0)
        if len(bits) == 2 and len(self.held) == 1:
            whole_rows = self.held[0]
            self.held = [whole_rows[:, :, :D // 2], whole_rows[:, :, D // 2:]]
            self.offsets = self.offsets * 2
        self.bits = bits
        self.got = [swap(h, bit, self.devices) for h, bit in zip(self.held, bits)]

    def take(self):
        if not self.turns:
            return (*self.held, *self.got), tuple((a, b, self.core) for a, b in zip(*self.offsets))
        self.held = [jnp.concatenate(pair) for pair in zip(self.held, self.got)]
        self.offsets = [o + [x ^ bit for x in o] for o, bit in zip(self.offsets, self.bits)]


def gather_small(shard, me, wide, narrow):
    devices = wide * narrow
    held = shard[None]
    bit = 1
    while bit < devices:
        held = jnp.concatenate([held, swap(held, bit, devices)])
        bit *= 2
    bit = 1
    while bit < devices:
        split = held.reshape(devices // (2 * bit), 2, bit, *shard.shape)
        held = jnp.where((me & bit) != 0, split[:, ::-1], split).reshape(held.shape)
        bit *= 2
    return held


def part(value, me, bit, axis, mine):
    index = (me & bit) != 0
    index = index.astype(jnp.int32) if mine else 1 - index.astype(jnp.int32)
    return lax.dynamic_index_in_dim(value, index, axis, keepdims=False)


def add(a, b, kind=BF16):
    return (a.astype(F32) + b.astype(F32)).astype(kind)


class Scatter:
    def __init__(self, me, wide, narrow):
        self.me, self.devices, self.narrow = me, wide * narrow, narrow
        self.inner, outer, _ = bit_steps(wide, narrow)
        self.orders = [list(outer), list(outer)[::-1]]
        self.turns = len(outer) + len(self.inner)
        self.done = 0

    def begin(self, mine, got):
        total = add(mine, got)
        width = len(self.orders[0])
        self.values = [h.reshape((2,) * width + h.shape[1:]) for h in (total[:, :, :D // 2], total[:, :, D // 2:])]
        self.split()

    def split(self):
        turn, outer = self.done, len(self.orders[0])
        if turn < outer:
            bits = [o[turn] for o in self.orders]
            axes = [sorted(o[turn:], reverse=True).index(bit) for o, bit in zip(self.orders, bits)]
        else:
            if turn == outer:
                self.values = [jnp.concatenate(self.values, axis=1)]
                self.values = [v.reshape(self.narrow, -1, D) for v in self.values]
            bits, axes = [self.inner[turn - outer]], [1]
            v = self.values[0]
            self.values = [v.reshape(v.shape[0] // 2, 2, *v.shape[1:])]
        self.bits = bits
        self.sends = [part(v, self.me, bit, axis, False) for v, bit, axis in zip(self.values, bits, axes)]
        self.keeps = [part(v, self.me, bit, axis, True) for v, bit, axis in zip(self.values, bits, axes)]

    def turn(self):
        self.got = [swap(s, bit, self.devices) for s, bit in zip(self.sends, self.bits)]

    def take(self):
        self.done += 1
        last = self.done == self.turns
        self.values = [add(a, b, F32 if last else BF16) for a, b in zip(self.keeps, self.got)]
        if last:
            return self.values[0][0]
        self.split()

    def over(self, inputs, work):
        self.sends, inputs = tie(self.sends, inputs)
        self.turn()
        result = work(inputs)
        self.got, result = tie(self.got, result)
        return result, self.take()


def scatter_small(grad, me, wide, narrow):
    devices = wide * narrow
    bit = devices // 2
    while bit:
        both = grad.reshape(2, bit, *grad.shape[1:])
        grad = add(part(both, me, bit, 0, True), swap(part(both, me, bit, 0, False), bit, devices), F32)
        bit //= 2
    return grad[0]


def split_grads(me, lhs, rhs, wide, narrow, owned):
    rows, side = narrow * owned, (me // narrow) % 2
    sides = [(1 - side).reshape(1).astype(jnp.int32), side.reshape(1).astype(jnp.int32)]
    if rows % 128 == 0:
        sent = dw(sides[0], lhs, rhs, rows, wide // 2)
        sent, lhs = tie(sent, lhs)
        got = swap(sent, narrow, wide * narrow)
        mine = dw(sides[1], lhs, rhs, rows, wide // 2)
        return mine, got
    repeats = rhs.shape[0] // lhs.shape[0]
    left = [lhs[0]] * 3 + [lhs[1]] if repeats == 2 else list(lhs)
    grad = jnp.concatenate([tn(a, b) for a, b in zip(left, rhs)], axis=0).astype(BF16)
    grad = grad.reshape(wide // 2, 2, rows, D)
    return part(grad, me, narrow, 1, True), swap(part(grad, me, narrow, 1, False), narrow, wide * narrow)


def spread(seqs, shares):
    runs, at = [], 0
    for j, share in enumerate(shares):
        upto = seqs * sum(shares[:j + 1]) // sum(shares)
        if upto > at:
            runs.append((at, upto - at))
        at = upto
    return runs


def forward_by_permutes(me, wide, narrow, tokens, seg, feat, attention, feedforward, vector):
    seqs = seg.shape[0]
    me1 = me.reshape(1).astype(jnp.int32)
    small = gather_small(vector, me, wide, narrow)
    vec = jnp.pad(jnp.transpose(small, (1, 0, 2)).reshape(small.shape[1], D).astype(F32), ((0, 3), (0, 0)))
    near = Gather(attention, wide, narrow)
    far = Gather(feedforward, wide, narrow)
    ready = narrow.bit_length() - 2
    early = len(far.turns) - 3
    for t in range(len(near.turns)):
        near.turn()
        behind = t > ready and early > 0
        if behind:
            far.turn()
            early -= 1
        near.got, far.held = tie(near.got, far.held)
        if behind:
            near.got, far.got = tie(near.got, far.got)
            far.take()
        weights = near.take()
    att, offsets = weights
    held = ()
    runs = spread(seqs, (1, 2, 1))
    for first_seq, count in runs:
        more = len(far.turns) > 0
        if more:
            far.held, source = tie(far.held, held if held else att)
            far.turn()
        else:
            source = held if held else att
        if held:
            *held, natural = *k1(first_seq, count, me1, tokens, seg, feat, [natural], offsets, vec, source), natural
        else:
            *held, natural = k1(first_seq, count, me1, tokens, seg, feat, source, offsets, vec, ())
        held = tuple(held)
        if more:
            far.got, held = tie(far.got, held)
            ff = far.take()
    while far.turns:
        far.turn()
        ff = far.take()
    ff = ff[0]
    return (*held, vec, natural, ff, offsets)


def local(wide, narrow, tokens, cotangent, segment_ids, feature_ids,
          attention_master, attention_first, attention_second,
          feedforward_master, feedforward_first, feedforward_second,
          vector_master, vector_first, vector_second):
    devices = wide * narrow
    me = lax.axis_index(BOTH)
    me1 = me.reshape(1).astype(jnp.int32)
    seg, feat = segment_ids, feature_ids
    seqs = seg.shape[0]
    shards = [m.astype(BF16) for m in (attention_master, feedforward_master, vector_master)]
    if devices <= 32:
        *held, vec, natural, ff = gathering_k1(wide, narrow, tokens, seg, feat, *shards)
        ff, offsets = [ff], ()
    else:
        *held, vec, natural, ff, offsets = forward_by_permutes(me, wide, narrow, tokens, seg, feat, *shards)
    mixed, q, k, v, ctx, lse = held
    out, first, fb, dctx, broad, slim, vg2 = k2(me1, mixed, ctx, cotangent, natural, ff, offsets, vec)
    ff_sum = Scatter(me, wide, narrow)
    ff_sum.begin(*split_grads(me, broad, slim, wide, narrow, feedforward_master.shape[0]))
    vg3, held, ff_owned = 0.0, (), None
    for first_seq, count in spread(seqs, (2, 1, 1)):
        def attend(given):
            source, kept = given
            return k3(first_seq, count, *source, ctx, dctx, fb, lse, seg, kept)
        (grads, more), ff_owned = ff_sum.over(((q, k, v), held), attend)
        held, vg3 = (grads,), vg3 + more
    d = held[0]
    if ff_owned is None:
        (mine, got), ff_owned = ff_sum.over((ctx, d), lambda g: split_grads(me, *g, wide, narrow, attention_master.shape[0]))
    else:
        mine, got = split_grads(me, ctx, d, wide, narrow, attention_master.shape[0])
    while ff_owned is None:
        _, ff_owned = ff_sum.over((), lambda g: ())
    att_sum = Scatter(me, wide, narrow)
    att_sum.begin(mine, got)
    vg4, held, att_owned = 0.0, (), None
    for first_seq, count in spread(seqs, (2, 1, 1)):
        def back(given):
            source, kept = given
            return k4(first_seq, count, source, d, tokens, seg, feat, natural, vec, kept)
        (grads, more), att_owned = att_sum.over((first, held), back)
        held, vg4 = (grads,), vg4 + more
    token_grads = held[0]
    vec_grad = jnp.concatenate([vg4[0:1], vg3[0:2], vg2[:10]], axis=0)
    vec_owned = scatter_small(jnp.transpose(vec_grad.reshape(vec_grad.shape[0], devices, -1), (1, 0, 2)), me, wide, narrow)
    while att_owned is None:
        att_sum.turn()
        att_owned = att_sum.take()
    ff_rate = rates(feedforward_master.shape[0], FF, D ** (-0.5), FF ** (-0.5))
    att_rate = rates(attention_master.shape[0], 3 * D, D ** (-0.5), (D // 64) ** (-0.5))
    f_new = adam_step(feedforward_master, feedforward_first, feedforward_second, ff_owned, ff_rate)
    a_new = adam_step(attention_master, attention_first, attention_second, att_owned, att_rate)
    v_new = adam_step(vector_master, vector_first, vector_second, vec_owned, VECTOR_RATE)
    result = [out, token_grads]
    for new in (a_new, f_new, v_new):
        result += [*new, new[0].astype(BF16)]
    return tuple(result)


def solution(mesh):
    rows, cols = P(BOTH, None), P(None, BOTH)
    return jax.shard_map(
        partial(local, mesh.shape["wide"], mesh.shape["narrow"]), mesh=mesh,
        in_specs=(rows,) * 10 + (cols,) * 3,
        out_specs=(rows,) * 10 + (cols,) * 4,
        check_vma=False,
    )
```

profile of v0, /device:TPU:0, one launch (start us, length us, event | category | flops | bytes accessed | tf_op | source)
XLA Modules:
  0.0 391.4 jit_solution(2712589381277116409)
XLA Ops:
  2.3 1.8 convert_element_type.219.ff_ref
  5.4 92.2 %gather_attend.1 = (f32[2048,768]{1,0:T(8,128)}, bf16[2048,768]{1,0:T(8,128)(2,1)}, bf16[2048,768]{1,0:T(8,128)(2,1)}, bf16[2048,768]{1,0:T(8,128)(2,1)}, bf16[2...) custom-call(bf16[2048,768]{1,0:T(8,128)(2,1)} %tok_ref.7, ...), custom_call_target="tpu_custom_call" | custom-call | flops 60000002048 | bytes 60000000 | tf_op jit(solution)/shard_map/gather_attend/pallas_call | solution.py:362
  97.6 84.3 %feed_forward.1 = (bf16[2048,768]{1,0:T(8,128)(2,1)}, f32[2048,768]{1,0:T(8,128)}, bf16[2048,768]{1,0:T(8,128)(2,1)}, bf16[2048,768]{1,0:T(8,128)(2,1)}, bf16[2,...) custom-call(s32[1]{0:T(128)} %bitcast.self_ref, ...), custom_call_target="tpu_custom_call" | custom-call | flops 60000002048 | bytes 80000000 | tf_op jit(solution)/shard_map/feed_forward/pallas_call | solution.py:448
  181.9 16.6 %weight_grad.4 = bf16[4,768,768]{2,1,0:T(8,128)(2,1)} custom-call(s32[1]{0:T(128)} %bitcast.2.side_ref, bf16[2,2048,3072]{2,1,0:T(8,128)(2,1)} %get-tuple-element.108.lhs_ref, bf16[2,2048,768]{2,1,0:T(8,128)(2,1)} %get-tuple-element.107.rhs_ref), custom_call_target="tpu_custom_call" | custom-call | flops 9663676416 | bytes 10000000 | tf_op jit(solution)/shard_map/weight_grad/pallas_call | solution.py:481
  198.9 16.8 %weight_grad.5 = bf16[4,768,768]{2,1,0:T(8,128)(2,1)} custom-call(s32[1]{0:T(128)} %bitcast.1.side_ref, bf16[2,2048,3072]{2,1,0:T(8,128)(2,1)} %get-tuple-element.108.lhs_ref, bf16[2,2048,768]{2,1,0:T(8,128)(2,1)} %get-tuple-element.107.rhs_ref), custom_call_target="tpu_custom_call" | custom-call | flops 9663676416 | bytes 10000000 | tf_op jit(solution)/shard_map/weight_grad/pallas_call | solution.py:481
  215.7 4.9 %add_convert_fusion = bf16[4,768,768]{2,1,0:T(8,128)(2,1)S(1)} fusion(bf16[4,768,768]{2,1,0:T(8,128)(2,1)} %collective-permute-done, bf16[4,768,768]{2,1,0:T(8,128)(2,1)} %weight_grad.5), kind=kLoop, calls=%fused_computation | loop fusion | flops 9437184 | bytes 14155776 | tf_op jit(solution)/shard_map/convert_element_type | solution.py:676
  224.5 27.4 %attend_back.3 = (bf16[4,2048,768]{2,1,0:T(8,128)(2,1)}, f32[8,768]{1,0:T(8,128)}) custom-call(bf16[2048,768]{1,0:T(8,128)(2,1)} %get-tuple-element.138.q_ref, bf16[2048,768]{1,0:T(8,128)(2,1)} %get-tuple-element.139.k_ref, bf16[2048,768]{1,0:T(8,128)(2,1)} %get-tuple-element.140.v_ref, bf16[2,2048,768]{2,1,0:T(8,128)(2,1)} %get-tuple-element.149.ctx_ref.lhs_ref, ...), custom_call_target="tpu_custom_call" | custom-call | flops 24000000000 | bytes 12000000 | tf_op jit(solution)/shard_map/attend_back/pallas_call | solution.py:544
  251.9 2.6 fusion
  258.0 15.3 %attend_back.4 = (bf16[4,2048,768]{2,1,0:T(8,128)(2,1)}, f32[8,768]{1,0:T(8,128)}) custom-call(bf16[2048,768]{1,0:T(8,128)(2,1)} %get-tuple-element.138.q_ref, bf16[2048,768]{1,0:T(8,128)(2,1)} %get-tuple-element.139.k_ref, bf16[2048,768]{1,0:T(8,128)(2,1)} %get-tuple-element.140.v_ref, ...), custom_call_target="tpu_custom_call", output_to_operand_aliasing={{0}: (8, {})} | custom-call | flops 12000000000 | bytes 6000000 | tf_op jit(solution)/shard_map/attend_back/pallas_call | solution.py:544
  276.0 15.3 %attend_back.5 = (bf16[4,2048,768]{2,1,0:T(8,128)(2,1)}, f32[8,768]{1,0:T(8,128)}) custom-call(bf16[2048,768]{1,0:T(8,128)(2,1)} %get-tuple-element.138.q_ref, bf16[2048,768]{1,0:T(8,128)(2,1)} %get-tuple-element.139.k_ref, bf16[2048,768]{1,0:T(8,128)(2,1)} %get-tuple-element.140.v_ref, ...), custom_call_target="tpu_custom_call", output_to_operand_aliasing={{0}: (8, {})} | custom-call | flops 12000000000 | bytes 6000000 | tf_op jit(solution)/shard_map/attend_back/pallas_call | solution.py:544
  291.5 11.8 %weight_grad.6 = bf16[4,384,768]{2,1,0:T(8,128)(2,1)} custom-call(s32[1]{0:T(128)} %bitcast.2.side_ref, bf16[2,2048,768]{2,1,0:T(8,128)(2,1)} %get-tuple-element.149.ctx_ref.lhs_ref, bf16[4,2048,768]{2,1,0:T(8,128)(2,1)} %get-tuple-element.148.rhs_ref.d_ref), custom_call_target="tpu_custom_call" | custom-call | flops 4831838208 | bytes 10000000 | tf_op jit(solution)/shard_map/weight_grad/pallas_call | solution.py:481
  304.7 11.6 %weight_grad.7 = bf16[4,384,768]{2,1,0:T(8,128)(2,1)} custom-call(s32[1]{0:T(128)} %bitcast.1.side_ref, bf16[2,2048,768]{2,1,0:T(8,128)(2,1)} %get-tuple-element.149.ctx_ref.lhs_ref, bf16[4,2048,768]{2,1,0:T(8,128)(2,1)} %get-tuple-element.148.rhs_ref.d_ref), custom_call_target="tpu_custom_call" | custom-call | flops 4831838208 | bytes 10000000 | tf_op jit(solution)/shard_map/weight_grad/pallas_call | solution.py:481
  316.3 3.7 collective-permute-done.6
  320.0 2.3 add_convert_fusion.1
  325.2 11.5 %token_grad.3 = (bf16[2048,768]{1,0:T(8,128)(2,1)}, f32[8,768]{1,0:T(8,128)}) custom-call(f32[2048,768]{1,0:T(8,128)} %get-tuple-element.172.first_ref, bf16[4,2048,768]{2,1,0:T(8,128)(2,1)} %get-tuple-element.148.rhs_ref.d_ref, bf16[2048,768]{1,0:T(8,128)(2,1)} %tok_ref.7, s32[4,512]{1,0:T(4,128)} %seg_ref.13, s32[4,512]{1,0:T(4,128)} %feat_ref.7, ...), custom_call_target="tpu_custom_call" | custom-call | flops 6000000000 | bytes 10000000 | tf_op jit(solution)/shard_map/token_grad/pallas_call | solution.py:582
  336.7 2.1 collective-permute-done.8
  343.6 7.8 %token_grad.4 = (bf16[2048,768]{1,0:T(8,128)(2,1)}, f32[8,768]{1,0:T(8,128)}) custom-call(f32[2048,768]{1,0:T(8,128)} %get-tuple-element.172.first_ref, bf16[4,2048,768]{2,1,0:T(8,128)(2,1)} %get-tuple-element.148.rhs_ref.d_ref, bf16[2048,768]{1,0:T(8,128)(2,1)} %tok_ref.7, s32[4,512]{1,0:T(4,128)} %seg_ref.13, ...), custom_call_target="tpu_custom_call", output_to_operand_aliasing={{0}: (7, {})} | custom-call | flops 3000000000 | bytes 5000000 | tf_op jit(solution)/shard_map/token_grad/pallas_call | solution.py:582
  352.5 7.9 %token_grad.5 = (bf16[2048,768]{1,0:T(8,128)(2,1)}, f32[8,768]{1,0:T(8,128)}) custom-call(f32[2048,768]{1,0:T(8,128)} %get-tuple-element.172.first_ref, bf16[4,2048,768]{2,1,0:T(8,128)(2,1)} %get-tuple-element.148.rhs_ref.d_ref, bf16[2048,768]{1,0:T(8,128)(2,1)} %tok_ref.7, s32[4,512]{1,0:T(4,128)} %seg_ref.13, ...), custom_call_target="tpu_custom_call", output_to_operand_aliasing={{0}: (7, {})} | custom-call | flops 3000000000 | bytes 5000000 | tf_op jit(solution)/shard_map/token_grad/pallas_call | solution.py:582
  363.7 3.4 collective-permute-done.14
  368.2 3.2 collective-permute-done.15
  371.6 2.8 fusion.18
  374.4 3.1 collective-permute-start.17
  379.3 1.9 collective-permute-start.18
  383.6 6.2 %collective-permute-done.13 = bf16[1,96,768]{2,1,0:T(8,128)(2,1)S(1)} collective-permute-done((bf16[1,96,768]{2,1,0:T(8,128)(2,1)S(1)}, bf16[1,96,768]{2,1,0:T(8,128)(2,1)S(1)}, u32[]{:S(2)}, u32[]{:S(2)}) %collective-permute-start.13) | collective-permute-done | bytes 147488 | tf_op jit(solution)/shard_map/ppermute | solution.py:628
  (106 shorter events, 33.8 us)
Async XLA Ops:
  198.5 17.2 %collective-permute-start = (bf16[4,768,768]{2,1,0:T(8,128)(2,1)}, bf16[4,768,768]{2,1,0:T(8,128)(2,1)}, u32[]{:S(2)}, u32[]{:S(2)}) collective-permute-start(bf16[4,768,768]{2,1,0:T(8,128)(2,1)} %weight_grad.4), channel_id=1, source_target_pairs={{0,4},{1,5},{2,6},{3,7},{4,0},{5,1},{6,2},{7,3},{8,12},{9,13},{10,... | collective-permute-start | bytes 14155784 | tf_op jit(solution)/shard_map/ppermute | solution.py:628
  222.9 29.0 %collective-permute-start.1 = (bf16[2,768,384]{2,1,0:T(8,128)(2,1)}, bf16[2,768,384]{2,1,0:T(8,128)(2,1)}, u32[]{:S(2)}, u32[]{:S(2)}) collective-permute-start(bf16[2,768,384]{2,1,0:T(8,128)(2,1)} %dynamic-slice_bitcast_fusion.1), channel_id=1, source_target_pairs={{0,8},{1,9},{2,10},{3,11},{4,12},{5,13},{6,14},{7,15},{8,0},{9,1},... | collective-permute-start | bytes 3538952 | tf_op jit(solution)/shard_map/ppermute | solution.py:628
  223.6 28.2 %collective-permute-start.2 = (bf16[2,768,384]{2,1,0:T(8,128)(2,1)S(1)}, bf16[2,768,384]{2,1,0:T(8,128)(2,1)}, u32[]{:S(2)}, u32[]{:S(2)}) collective-permute-start(bf16[2,768,384]{2,1,0:T(8,128)(2,1)S(1)} %dynamic-slice_bitcast_fusion), channel_id=1, source_target_pairs={{0,16},{1,17},{2,18},{3,19},{4,20},{5,21},{6,22},{7,23},{8,24},{9,... | collective-permute-start | bytes 3538952 | tf_op jit(solution)/shard_map/ppermute | solution.py:628
  255.6 17.7 %collective-permute-start.3 = (bf16[768,384]{1,0:T(8,128)(2,1)S(1)}, bf16[768,384]{1,0:T(8,128)(2,1)}, u32[]{:S(2)}, u32[]{:S(2)}) collective-permute-start(bf16[768,384]{1,0:T(8,128)(2,1)S(1)} %dynamic-slice_bitcast_fusion.6), channel_id=1, source_target_pairs={{0,16},{1,17},{2,18},{3,19},{4,20},{5,21},{6,22},{7,23},{8,24},{9,... | collective-permute-start | bytes 1769480 | tf_op jit(solution)/shard_map/ppermute | solution.py:628
  256.8 16.5 %collective-permute-start.4 = (bf16[768,384]{1,0:T(8,128)(2,1)S(1)}, bf16[768,384]{1,0:T(8,128)(2,1)}, u32[]{:S(2)}, u32[]{:S(2)}) collective-permute-start(bf16[768,384]{1,0:T(8,128)(2,1)S(1)} %dynamic-slice_bitcast_fusion.5), channel_id=1, source_target_pairs={{0,8},{1,9},{2,10},{3,11},{4,12},{5,13},{6,14},{7,15},{8,0},{9,1},... | collective-permute-start | bytes 1769480 | tf_op jit(solution)/shard_map/ppermute | solution.py:628
  275.9 15.4 %collective-permute-start.5 = (bf16[2,192,768]{2,1,0:T(8,128)(2,1)S(1)}, bf16[2,192,768]{2,1,0:T(8,128)(2,1)S(1)}, u32[]{:S(2)}, u32[]{:S(2)}) collective-permute-start(bf16[2,192,768]{2,1,0:T(8,128)(2,1)S(1)} %dynamic-slice_bitcast_fusion.4), channel_id=1, source_target_pairs={{0,1},{1,0},{2,3},{3,2},{4,5},{5,4},{6,7},{7,6},{8,9},{9,8},{10,11... | collective-permute-start | bytes 1769480 | tf_op jit(solution)/shard_map/ppermute | solution.py:628
  303.3 16.6 %collective-permute-start.7 = (bf16[4,384,768]{2,1,0:T(8,128)(2,1)}, bf16[4,384,768]{2,1,0:T(8,128)(2,1)S(1)}, u32[]{:S(2)}, u32[]{:S(2)}) collective-permute-start(bf16[4,384,768]{2,1,0:T(8,128)(2,1)} %weight_grad.6), channel_id=1, source_target_pairs={{0,4},{1,5},{2,6},{3,7},{4,0},{5,1},{6,2},{7,3},{8,12},{9,13},{10,... | collective-permute-start | bytes 7077896 | tf_op jit(solution)/shard_map/ppermute | solution.py:628
  303.3 16.6 %collective-permute-start.6 = (bf16[1,192,768]{2,1,0:T(8,128)(2,1)S(1)}, bf16[1,192,768]{2,1,0:T(8,128)(2,1)S(1)}, u32[]{:S(2)}, u32[]{:S(2)}) collective-permute-start(bf16[1,192,768]{2,1,0:T(8,128)(2,1)S(1)} %constant_dynamic-slice_fusion.5), channel_id=1, source_target_pairs={{0,2},{1,3},{2,0},{3,1},{4,6},{5,7},{6,4},{7,5},{8,10},{9,11},{10,... | collective-permute-start | bytes 884744 | tf_op jit(solution)/shard_map/ppermute | solution.py:628
  323.5 15.3 %collective-permute-start.8 = (bf16[2,384,384]{2,1,0:T(8,128)(2,1)}, bf16[2,384,384]{2,1,0:T(8,128)(2,1)}, u32[]{:S(2)}, u32[]{:S(2)}) collective-permute-start(bf16[2,384,384]{2,1,0:T(8,128)(2,1)} %dynamic-slice_bitcast_fusion.3), channel_id=1, source_target_pairs={{0,8},{1,9},{2,10},{3,11},{4,12},{5,13},{6,14},{7,15},{8,0},{9,1},... | collective-permute-start | bytes 1769480 | tf_op jit(solution)/shard_map/ppermute | solution.py:628
  324.3 14.7 %collective-permute-start.9 = (bf16[2,384,384]{2,1,0:T(8,128)(2,1)S(1)}, bf16[2,384,384]{2,1,0:T(8,128)(2,1)}, u32[]{:S(2)}, u32[]{:S(2)}) collective-permute-start(bf16[2,384,384]{2,1,0:T(8,128)(2,1)S(1)} %dynamic-slice_bitcast_fusion.2), channel_id=1, source_target_pairs={{0,16},{1,17},{2,18},{3,19},{4,20},{5,21},{6,22},{7,23},{8,24},{9,... | collective-permute-start | bytes 1769480 | tf_op jit(solution)/shard_map/ppermute | solution.py:628
  341.5 9.8 %collective-permute-start.10 = (bf16[384,384]{1,0:T(8,128)(2,1)S(1)}, bf16[384,384]{1,0:T(8,128)(2,1)S(1)}, u32[]{:S(2)}, u32[]{:S(2)}) collective-permute-start(bf16[384,384]{1,0:T(8,128)(2,1)S(1)} %dynamic-slice_bitcast_fusion.9), channel_id=1, source_target_pairs={{0,16},{1,17},{2,18},{3,19},{4,20},{5,21},{6,22},{7,23},{8,24},{9,... | collective-permute-start | bytes 884744 | tf_op jit(solution)/shard_map/ppermute | solution.py:628
  342.5 8.8 %collective-permute-start.11 = (bf16[384,384]{1,0:T(8,128)(2,1)S(1)}, bf16[384,384]{1,0:T(8,128)(2,1)S(1)}, u32[]{:S(2)}, u32[]{:S(2)}) collective-permute-start(bf16[384,384]{1,0:T(8,128)(2,1)S(1)} %dynamic-slice_bitcast_fusion.8), channel_id=1, source_target_pairs={{0,8},{1,9},{2,10},{3,11},{4,12},{5,13},{6,14},{7,15},{8,0},{9,1},... | collective-permute-start | bytes 884744 | tf_op jit(solution)/shard_map/ppermute | solution.py:628
  351.7 8.8 %collective-permute-start.12 = (bf16[2,96,768]{2,1,0:T(8,128)(2,1)S(1)}, bf16[2,96,768]{2,1,0:T(8,128)(2,1)S(1)}, u32[]{:S(2)}, u32[]{:S(2)}) collective-permute-start(bf16[2,96,768]{2,1,0:T(8,128)(2,1)S(1)} %dynamic-slice_bitcast_fusion.7), channel_id=1, source_target_pairs={{0,1},{1,0},{2,3},{3,2},{4,5},{5,4},{6,7},{7,6},{8,9},{9,8},{10,11... | collective-permute-start | bytes 884744 | tf_op jit(solution)/shard_map/ppermute | solution.py:628
  352.5 19.0 %copy-start.3 = (f32[192,768]{1,0:T(8,128)S(1)}, f32[192,768]{1,0:T(8,128)}, u32[]{:S(2)}) copy-start(f32[192,768]{1,0:T(8,128)} %param.20) | copy-start | bytes 1769476
  352.5 19.0 %copy-start.5 = (f32[192,768]{1,0:T(8,128)S(1)}, f32[192,768]{1,0:T(8,128)}, u32[]{:S(2)}) copy-start(f32[192,768]{1,0:T(8,128)} %param.21) | copy-start | bytes 1769476
  352.5 19.0 %copy-start.6 = (f32[192,768]{1,0:T(8,128)S(1)}, f32[192,768]{1,0:T(8,128)}, u32[]{:S(2)}) copy-start(f32[192,768]{1,0:T(8,128)} %param.22) | copy-start | bytes 1769476
  362.3 4.8 %collective-permute-start.14 = (f32[16,13,24]{2,0,1:T(8,128)S(1)}, f32[16,13,24]{2,0,1:T(8,128)S(1)}, u32[]{:S(2)}, u32[]{:S(2)}) collective-permute-start(f32[16,13,24]{2,0,1:T(8,128)S(1)} %dynamic-slice_bitcast_fusion.10), channel_id=1, source_target_pairs={{0,16},{1,17},{2,18},{3,19},{4,20},{5,21},{6,22},{7,23},{8,24},{9,... | collective-permute-start | bytes 59912 | tf_op jit(solution)/shard_map/ppermute | solution.py:628
  367.1 4.2 %collective-permute-start.15 = (f32[8,13,24]{2,0,1:T(8,128)S(1)}, f32[8,13,24]{2,0,1:T(8,128)S(1)}, u32[]{:S(2)}, u32[]{:S(2)}) collective-permute-start(f32[8,13,24]{2,0,1:T(8,128)S(1)} %dynamic-slice_bitcast_fusion.11), channel_id=1, source_target_pairs={{0,8},{1,9},{2,10},{3,11},{4,12},{5,13},{6,14},{7,15},{8,0},{9,1},... | collective-permute-start | bytes 29960 | tf_op jit(solution)/shard_map/ppermute | solution.py:628
  371.4 18.4 %copy-start.4 = (f32[96,768]{1,0:T(8,128)S(1)}, f32[96,768]{1,0:T(8,128)}, u32[]{:S(2)}) copy-start(f32[96,768]{1,0:T(8,128)} %param.17) | copy-start | bytes 884740
  371.4 18.4 %copy-start.10 = (f32[96,768]{1,0:T(8,128)S(1)}, f32[96,768]{1,0:T(8,128)}, u32[]{:S(2)}) copy-start(f32[96,768]{1,0:T(8,128)} %param.18) | copy-start | bytes 884740
  371.4 2.9 collective-permute-start.16
  374.4 4.9 %collective-permute-start.17 = (f32[2,13,24]{2,1,0:T(8,128)S(1)}, f32[2,13,24]{2,1,0:T(8,128)S(1)}, u32[]{:S(2)}, u32[]{:S(2)}) collective-permute-start(f32[2,13,24]{2,1,0:T(8,128)S(1)} %bitcast.130), channel_id=1, source_target_pairs={{0,2},{1,3},{2,0},{3,1},{4,6},{5,7},{6,4},{7,5},{8,10},{9,11},{10,... | collective-permute-start | bytes 7496 | tf_op jit(solution)/shard_map/ppermute | solution.py:628
  379.3 3.7 collective-permute-start.18
  381.2 8.7 %collective-permute-start.13 = (bf16[1,96,768]{2,1,0:T(8,128)(2,1)S(1)}, bf16[1,96,768]{2,1,0:T(8,128)(2,1)S(1)}, u32[]{:S(2)}, u32[]{:S(2)}) collective-permute-start(bf16[1,96,768]{2,1,0:T(8,128)(2,1)S(1)} %constant_dynamic-slice_fusion.4), channel_id=1, source_target_pairs={{0,2},{1,3},{2,0},{3,1},{4,6},{5,7},{6,4},{7,5},{8,10},{9,11},{10,... | collective-permute-start | bytes 442376 | tf_op jit(solution)/shard_map/ppermute | solution.py:628
  (10 other events, 83.1 us)
where the time goes:
time: 397 us; the launch traced here: 391 us
  Pallas kernels  318 us (80%)
  other arithmetic  26.5 us (7%)
  waiting for transfers between devices  21.1 us (5%)
  starting transfers between devices  18.6 us (5%)
  local copies, waits for them, and re-layouts  5.6 us (1%)
    pallas_call x1, Pallas kernels, gathering_k1(): pl.pallas_call(partial(gathering_k1_body, wide, narrow, vec_shard.shape[1...  92.2 us
    pallas_call x1, Pallas kernels, k2(): pl.pallas_call(partial(k2_body, offsets), grid_spec=pltpu.PrefetchScalarG...  84.3 us
    pallas_call x3, Pallas kernels, k3(): pl.pallas_call(partial(k3_body, first_seq, len(kept)), grid=(count,), in_...  57.9 us
    pallas_call x4, Pallas kernels, dw(): pl.pallas_call(partial(dw_body, rows), grid_spec=pltpu.PrefetchScalarGrid...  56.8 us
    pallas_call x3, Pallas kernels, k4(): pl.pallas_call(partial(k4_body, first_seq, len(kept)), grid=(count,), in_...  27.1 us
    ppermute x19, waiting for transfers between devices, swap(): return lax.ppermute(value, BOTH, [(i, i ^ bit) for i in range(devices)])  21.1 us
    ppermute x19, starting transfers between devices, swap(): return lax.ppermute(value, BOTH, [(i, i ^ bit) for i in range(devices)])  18.6 us
    convert_element_type x11, other arithmetic, add(): return (a.astype(F32) + b.astype(F32)).astype(kind)  15 us
  transfers between devices with their start and end apart: 19, of which 8 were waited for; matrix products, arithmetic and copies ran while one was open for 1% of the time, Pallas kernels for 29%

commit v1 on v0

--- a/solution.py
+++ b/solution.py
@@ -30,15 +30,10 @@
     return pl.BlockSpec(shape, lambda *_: (0,) * len(shape), pipeline_mode=pl.Buffered(1))
 
 def gelu_pair(h):
-    size = jnp.abs(h)
-    t = 1.0 / (1.0 + (0.42 * 0.7071067811865476) * size)
+    below = 0.5 + 0.5 * lax.erf(h * 0.7071067811865476)
     bell = jnp.exp(h * h * -0.5)
-    poly = jnp.full_like(t, ERFC[-1])
-    for coef in ERFC[-2::-1]:
-        poly = poly * t + coef
-    tail = poly * t * bell
-    below = jnp.where(h < 0, tail, 1.0 - tail)
-    return h * below, below + h * bell * 0.3989422804014327
+    return h * below, below + h * (bell * 0.3989422804014327)
+
 
 def column_of(row):
     return jnp.transpose(jnp.broadcast_to(row, (8, row.shape[1])))[:, :1]
@@ -463,13 +458,9 @@
     )(me, mixed, ctx, cot, att, vec, *ff)
 
 def dw_body(rows, side_ref, lhs_ref, rhs_ref, out_ref):
-    step = 128 if rows % 256 else 256
-
-    def chunk(c, carry):
-        at = pl.ds(pl.multiple_of(c * step, step), step)
-        out_ref[0, at, :] = tn(lhs_ref[0, :, at], rhs_ref[0]).astype(BF16)
-        return carry
-    lax.fori_loop(0, rows // step, chunk, 0)
+    step = 384 if rows % 384 == 0 else 128
+    for at in range(0, rows, step):
+        out_ref[0, at:at + step, :] = tn(lhs_ref[0, :, at:at + step], rhs_ref[0]).astype(BF16)
 
 
 def dw(side, lhs, rhs, rows, count):
@@ -506,8 +497,9 @@
     bias_scr[...] = jnp.where(column_of(seg) == seg, 0.0, AWAY)
     lse_scr[...] = jnp.transpose(lse_ref[...])[:16, :]
     prod = dctx_ref[...].astype(F32) * ctx_ref[...].astype(F32)
-    pick = (lax.broadcasted_iota(jnp.int32, (16, D), 1) // HEAD_DIM == lax.broadcasted_iota(jnp.int32, (16, D), 0)).astype(F32)
-    del_scr[...] = lax.dot_general(pick, prod, (((1,), (1,)), ((), ())), precision=lax.Precision.HIGHEST, preferred_element_type=F32)
+    pick = (lax.broadcasted_iota(jnp.int32, (16, D), 1) // HEAD_DIM == lax.broadcasted_iota(jnp.int32, (16, D), 0)).astype(F32).astype(BF16)
+    high = prod.astype(BF16)
+    del_scr[...] = nt(pick, high) + nt(pick, (prod - high.astype(F32)).astype(BF16))
     low = lax.broadcasted_iota(jnp.int32, (length, 128), 1) < HEAD_DIM
 
     def pair(p, carry):

time: 397 us -> 375 us (0.945)
  Pallas kernels: 318 us -> 294 us
    pallas_call x1, Pallas kernels: 84.3 us -> 68.3 us  [k2(): pl.pallas_call(partial(k2_body, offsets), grid_spec=pltpu.PrefetchScalarG...]
    pallas_call x4, Pallas kernels: 56.8 us -> 51.2 us  [dw(): pl.pallas_call(partial(dw_body, rows), grid_spec=pltpu.PrefetchScalarGrid...]
  transfers between devices with their start and end apart: 19 -> 19, of which waited for: 8 -> 10; matrix products, arithmetic and copies ran while one was open for 1% -> 1% of each run, Pallas kernels for 29% -> 29%
where the time goes in v1:
time: 375 us; the launch traced here: 369 us
  Pallas kernels  294 us (78%)
  other arithmetic  26.4 us (7%)
  waiting for transfers between devices  24 us (6%)
  starting transfers between devices  18 us (5%)
  local copies, waits for them, and re-layouts  5.6 us (1%)
    pallas_call x1, Pallas kernels, gathering_k1(): pl.pallas_call(partial(gathering_k1_body, wide, narrow, vec_shard.shape[1...  92.2 us
    pallas_call x1, Pallas kernels, k2(): pl.pallas_call(partial(k2_body, offsets), grid_spec=pltpu.PrefetchScalarG...  68.3 us
    pallas_call x3, Pallas kernels, k3(): pl.pallas_call(partial(k3_body, first_seq, len(kept)), grid=(count,), in_...  54.8 us
    pallas_call x4, Pallas kernels, dw(): pl.pallas_call(partial(dw_body, rows), grid_spec=pltpu.PrefetchScalarGrid...  51.2 us
    pallas_call x3, Pallas kernels, k4(): pl.pallas_call(partial(k4_body, first_seq, len(kept)), grid=(count,), in_...  27.1 us
    ppermute x19, waiting for transfers between devices, swap(): return lax.ppermute(value, BOTH, [(i, i ^ bit) for i in range(devices)])  24 us
    ppermute x19, starting transfers between devices, swap(): return lax.ppermute(value, BOTH, [(i, i ^ bit) for i in range(devices)])  18 us
    convert_element_type x11, other arithmetic, add(): return (a.astype(F32) + b.astype(F32)).astype(kind)  15 us
  transfers between devices with their start and end apart: 19, of which 10 were waited for; matrix products, arithmetic and copies ran while one was open for 1% of the time, Pallas kernels for 29%

profile of v1, /device:TPU:0, one launch (start us, length us, event | category | flops | bytes accessed | tf_op | source)
XLA Modules:
  0.0 369.2 jit_solution(3324851644240408675)
XLA Ops:
  2.3 1.8 convert_element_type.219.ff_ref
  5.4 92.2 %gather_attend.1 = (f32[2048,768]{1,0:T(8,128)}, bf16[2048,768]{1,0:T(8,128)(2,1)}, bf16[2048,768]{1,0:T(8,128)(2,1)}, bf16[2048,768]{1,0:T(8,128)(2,1)}, bf16[2...) custom-call(bf16[2048,768]{1,0:T(8,128)(2,1)} %tok_ref.7, ...), custom_call_target="tpu_custom_call" | custom-call | flops 60000002048 | bytes 60000000 | tf_op jit(solution)/shard_map/gather_attend/pallas_call | solution.py:357
  97.6 68.3 %feed_forward.1 = (bf16[2048,768]{1,0:T(8,128)(2,1)}, f32[2048,768]{1,0:T(8,128)}, bf16[2048,768]{1,0:T(8,128)(2,1)}, bf16[2048,768]{1,0:T(8,128)(2,1)}, bf16[2,...) custom-call(s32[1]{0:T(128)} %bitcast.self_ref, ...), custom_call_target="tpu_custom_call" | custom-call | flops 60000002048 | bytes 80000000 | tf_op jit(solution)/shard_map/feed_forward/pallas_call | solution.py:443
  165.9 15.1 %weight_grad.4 = bf16[4,768,768]{2,1,0:T(8,128)(2,1)} custom-call(s32[1]{0:T(128)} %bitcast.2.side_ref, bf16[2,2048,3072]{2,1,0:T(8,128)(2,1)} %get-tuple-element.108.lhs_ref, bf16[2,2048,768]{2,1,0:T(8,128)(2,1)} %get-tuple-element.107.rhs_ref), custom_call_target="tpu_custom_call" | custom-call | flops 9663676416 | bytes 10000000 | tf_op jit(solution)/shard_map/weight_grad/pallas_call | solution.py:472
  181.4 15.3 %weight_grad.5 = bf16[4,768,768]{2,1,0:T(8,128)(2,1)} custom-call(s32[1]{0:T(128)} %bitcast.1.side_ref, bf16[2,2048,3072]{2,1,0:T(8,128)(2,1)} %get-tuple-element.108.lhs_ref, bf16[2,2048,768]{2,1,0:T(8,128)(2,1)} %get-tuple-element.107.rhs_ref), custom_call_target="tpu_custom_call" | custom-call | flops 9663676416 | bytes 10000000 | tf_op jit(solution)/shard_map/weight_grad/pallas_call | solution.py:472
  196.6 4.9 %add_convert_fusion = bf16[4,768,768]{2,1,0:T(8,128)(2,1)S(1)} fusion(bf16[4,768,768]{2,1,0:T(8,128)(2,1)} %collective-permute-done, bf16[4,768,768]{2,1,0:T(8,128)(2,1)} %weight_grad.5), kind=kLoop, calls=%fused_computation | loop fusion | flops 9437184 | bytes 14155776 | tf_op jit(solution)/shard_map/convert_element_type | solution.py:668
  205.4 25.8 %attend_back.3 = (bf16[4,2048,768]{2,1,0:T(8,128)(2,1)}, f32[8,768]{1,0:T(8,128)}) custom-call(bf16[2048,768]{1,0:T(8,128)(2,1)} %get-tuple-element.138.q_ref, bf16[2048,768]{1,0:T(8,128)(2,1)} %get-tuple-element.139.k_ref, bf16[2048,768]{1,0:T(8,128)(2,1)} %get-tuple-element.140.v_ref, bf16[2,2048,768]{2,1,0:T(8,128)(2,1)} %get-tuple-element.149.ctx_ref.lhs_ref, ...), custom_call_target="tpu_custom_call" | custom-call | flops 24000000000 | bytes 12000000 | tf_op jit(solution)/shard_map/attend_back/pallas_call | solution.py:536
  232.4 2.6 fusion
  238.1 14.5 %attend_back.4 = (bf16[4,2048,768]{2,1,0:T(8,128)(2,1)}, f32[8,768]{1,0:T(8,128)}) custom-call(bf16[2048,768]{1,0:T(8,128)(2,1)} %get-tuple-element.138.q_ref, bf16[2048,768]{1,0:T(8,128)(2,1)} %get-tuple-element.139.k_ref, bf16[2048,768]{1,0:T(8,128)(2,1)} %get-tuple-element.140.v_ref, ...), custom_call_target="tpu_custom_call", output_to_operand_aliasing={{0}: (8, {})} | custom-call | flops 12000000000 | bytes 6000000 | tf_op jit(solution)/shard_map/attend_back/pallas_call | solution.py:536
  255.3 14.5 %attend_back.5 = (bf16[4,2048,768]{2,1,0:T(8,128)(2,1)}, f32[8,768]{1,0:T(8,128)}) custom-call(bf16[2048,768]{1,0:T(8,128)(2,1)} %get-tuple-element.138.q_ref, bf16[2048,768]{1,0:T(8,128)(2,1)} %get-tuple-element.139.k_ref, bf16[2048,768]{1,0:T(8,128)(2,1)} %get-tuple-element.140.v_ref, ...), custom_call_target="tpu_custom_call", output_to_operand_aliasing={{0}: (8, {})} | custom-call | flops 12000000000 | bytes 6000000 | tf_op jit(solution)/shard_map/attend_back/pallas_call | solution.py:536
  270.0 10.3 %weight_grad.6 = bf16[4,384,768]{2,1,0:T(8,128)(2,1)} custom-call(s32[1]{0:T(128)} %bitcast.2.side_ref, bf16[2,2048,768]{2,1,0:T(8,128)(2,1)} %get-tuple-element.149.ctx_ref.lhs_ref, bf16[4,2048,768]{2,1,0:T(8,128)(2,1)} %get-tuple-element.148.rhs_ref.d_ref), custom_call_target="tpu_custom_call" | custom-call | flops 4831838208 | bytes 10000000 | tf_op jit(solution)/shard_map/weight_grad/pallas_call | solution.py:472
  281.6 10.5 %weight_grad.7 = bf16[4,384,768]{2,1,0:T(8,128)(2,1)} custom-call(s32[1]{0:T(128)} %bitcast.1.side_ref, bf16[2,2048,768]{2,1,0:T(8,128)(2,1)} %get-tuple-element.149.ctx_ref.lhs_ref, bf16[4,2048,768]{2,1,0:T(8,128)(2,1)} %get-tuple-element.148.rhs_ref.d_ref), custom_call_target="tpu_custom_call" | custom-call | flops 4831838208 | bytes 10000000 | tf_op jit(solution)/shard_map/weight_grad/pallas_call | solution.py:472
  292.1 4.9 %collective-permute-done.6 = bf16[1,192,768]{2,1,0:T(8,128)(2,1)S(1)} collective-permute-done((bf16[1,192,768]{2,1,0:T(8,128)(2,1)S(1)}, bf16[1,192,768]{2,1,0:T(8,128)(2,1)S(1)}, u32[]{:S(2)}, u32[]{:S(2)}) %collective-permute-start.6) | collective-permute-done | bytes 294944 | tf_op jit(solution)/shard_map/ppermute | solution.py:620
  297.0 2.3 add_convert_fusion.1
  302.6 11.5 %token_grad.3 = (bf16[2048,768]{1,0:T(8,128)(2,1)}, f32[8,768]{1,0:T(8,128)}) custom-call(f32[2048,768]{1,0:T(8,128)} %get-tuple-element.172.first_ref, bf16[4,2048,768]{2,1,0:T(8,128)(2,1)} %get-tuple-element.148.rhs_ref.d_ref, bf16[2048,768]{1,0:T(8,128)(2,1)} %tok_ref.7, s32[4,512]{1,0:T(4,128)} %seg_ref.13, s32[4,512]{1,0:T(4,128)} %feat_ref.7, ...), custom_call_target="tpu_custom_call" | custom-call | flops 6000000000 | bytes 10000000 | tf_op jit(solution)/shard_map/token_grad/pallas_call | solution.py:574
  314.1 1.7 collective-permute-done.8
  321.3 7.8 %token_grad.4 = (bf16[2048,768]{1,0:T(8,128)(2,1)}, f32[8,768]{1,0:T(8,128)}) custom-call(f32[2048,768]{1,0:T(8,128)} %get-tuple-element.172.first_ref, bf16[4,2048,768]{2,1,0:T(8,128)(2,1)} %get-tuple-element.148.rhs_ref.d_ref, bf16[2048,768]{1,0:T(8,128)(2,1)} %tok_ref.7, s32[4,512]{1,0:T(4,128)} %seg_ref.13, ...), custom_call_target="tpu_custom_call", output_to_operand_aliasing={{0}: (7, {})} | custom-call | flops 3000000000 | bytes 5000000 | tf_op jit(solution)/shard_map/token_grad/pallas_call | solution.py:574
  330.2 7.9 %token_grad.5 = (bf16[2048,768]{1,0:T(8,128)(2,1)}, f32[8,768]{1,0:T(8,128)}) custom-call(f32[2048,768]{1,0:T(8,128)} %get-tuple-element.172.first_ref, bf16[4,2048,768]{2,1,0:T(8,128)(2,1)} %get-tuple-element.148.rhs_ref.d_ref, bf16[2048,768]{1,0:T(8,128)(2,1)} %tok_ref.7, s32[4,512]{1,0:T(4,128)} %seg_ref.13, ...), custom_call_target="tpu_custom_call", output_to_operand_aliasing={{0}: (7, {})} | custom-call | flops 3000000000 | bytes 5000000 | tf_op jit(solution)/shard_map/token_grad/pallas_call | solution.py:574
  340.7 4.0 %collective-permute-done.14 = f32[16,13,24]{2,0,1:T(8,128)S(1)} collective-permute-done((f32[16,13,24]{2,0,1:T(8,128)S(1)}, f32[16,13,24]{2,0,1:T(8,128)S(1)}, u32[]{:S(2)}, u32[]{:S(2)}) %collective-permute-start.14) | collective-permute-done | bytes 20000 | tf_op jit(solution)/shard_map/ppermute | solution.py:620
  345.6 3.4 collective-permute-done.15
  349.2 2.8 fusion.18
  352.1 3.3 collective-permute-start.17
  357.1 1.6 collective-permute-start.18
  361.4 6.1 %collective-permute-done.13 = bf16[1,96,768]{2,1,0:T(8,128)(2,1)S(1)} collective-permute-done((bf16[1,96,768]{2,1,0:T(8,128)(2,1)S(1)}, bf16[1,96,768]{2,1,0:T(8,128)(2,1)S(1)}, u32[]{:S(2)}, u32[]{:S(2)}) %collective-permute-start.13) | collective-permute-done | bytes 147488 | tf_op jit(solution)/shard_map/ppermute | solution.py:620
  (106 shorter events, 34.6 us)
Async XLA Ops:
  181.0 15.6 %collective-permute-start = (bf16[4,768,768]{2,1,0:T(8,128)(2,1)}, bf16[4,768,768]{2,1,0:T(8,128)(2,1)}, u32[]{:S(2)}, u32[]{:S(2)}) collective-permute-start(bf16[4,768,768]{2,1,0:T(8,128)(2,1)} %weight_grad.4), channel_id=1, source_target_pairs={{0,4},{1,5},{2,6},{3,7},{4,0},{5,1},{6,2},{7,3},{8,12},{9,13},{10,... | collective-permute-start | bytes 14155784 | tf_op jit(solution)/shard_map/ppermute | solution.py:620
  203.8 28.3 %collective-permute-start.1 = (bf16[2,768,384]{2,1,0:T(8,128)(2,1)}, bf16[2,768,384]{2,1,0:T(8,128)(2,1)}, u32[]{:S(2)}, u32[]{:S(2)}) collective-permute-start(bf16[2,768,384]{2,1,0:T(8,128)(2,1)} %dynamic-slice_bitcast_fusion.1), channel_id=1, source_target_pairs={{0,8},{1,9},{2,10},{3,11},{4,12},{5,13},{6,14},{7,15},{8,0},{9,1},... | collective-permute-start | bytes 3538952 | tf_op jit(solution)/shard_map/ppermute | solution.py:620
  204.6 27.8 %collective-permute-start.2 = (bf16[2,768,384]{2,1,0:T(8,128)(2,1)S(1)}, bf16[2,768,384]{2,1,0:T(8,128)(2,1)}, u32[]{:S(2)}, u32[]{:S(2)}) collective-permute-start(bf16[2,768,384]{2,1,0:T(8,128)(2,1)S(1)} %dynamic-slice_bitcast_fusion), channel_id=1, source_target_pairs={{0,16},{1,17},{2,18},{3,19},{4,20},{5,21},{6,22},{7,23},{8,24},{9,... | collective-permute-start | bytes 3538952 | tf_op jit(solution)/shard_map/ppermute | solution.py:620
  236.1 16.6 %collective-permute-start.3 = (bf16[768,384]{1,0:T(8,128)(2,1)S(1)}, bf16[768,384]{1,0:T(8,128)(2,1)}, u32[]{:S(2)}, u32[]{:S(2)}) collective-permute-start(bf16[768,384]{1,0:T(8,128)(2,1)S(1)} %dynamic-slice_bitcast_fusion.6), channel_id=1, source_target_pairs={{0,16},{1,17},{2,18},{3,19},{4,20},{5,21},{6,22},{7,23},{8,24},{9,... | collective-permute-start | bytes 1769480 | tf_op jit(solution)/shard_map/ppermute | solution.py:620
  237.0 15.6 %collective-permute-start.4 = (bf16[768,384]{1,0:T(8,128)(2,1)S(1)}, bf16[768,384]{1,0:T(8,128)(2,1)}, u32[]{:S(2)}, u32[]{:S(2)}) collective-permute-start(bf16[768,384]{1,0:T(8,128)(2,1)S(1)} %dynamic-slice_bitcast_fusion.5), channel_id=1, source_target_pairs={{0,8},{1,9},{2,10},{3,11},{4,12},{5,13},{6,14},{7,15},{8,0},{9,1},... | collective-permute-start | bytes 1769480 | tf_op jit(solution)/shard_map/ppermute | solution.py:620
  255.3 14.6 %collective-permute-start.5 = (bf16[2,192,768]{2,1,0:T(8,128)(2,1)S(1)}, bf16[2,192,768]{2,1,0:T(8,128)(2,1)S(1)}, u32[]{:S(2)}, u32[]{:S(2)}) collective-permute-start(bf16[2,192,768]{2,1,0:T(8,128)(2,1)S(1)} %dynamic-slice_bitcast_fusion.4), channel_id=1, source_target_pairs={{0,1},{1,0},{2,3},{3,2},{4,5},{5,4},{6,7},{7,6},{8,9},{9,8},{10,11... | collective-permute-start | bytes 1769480 | tf_op jit(solution)/shard_map/ppermute | solution.py:620
  280.3 16.6 %collective-permute-start.7 = (bf16[4,384,768]{2,1,0:T(8,128)(2,1)}, bf16[4,384,768]{2,1,0:T(8,128)(2,1)S(1)}, u32[]{:S(2)}, u32[]{:S(2)}) collective-permute-start(bf16[4,384,768]{2,1,0:T(8,128)(2,1)} %weight_grad.6), channel_id=1, source_target_pairs={{0,4},{1,5},{2,6},{3,7},{4,0},{5,1},{6,2},{7,3},{8,12},{9,13},{10,... | collective-permute-start | bytes 7077896 | tf_op jit(solution)/shard_map/ppermute | solution.py:620
  280.3 16.6 %collective-permute-start.6 = (bf16[1,192,768]{2,1,0:T(8,128)(2,1)S(1)}, bf16[1,192,768]{2,1,0:T(8,128)(2,1)S(1)}, u32[]{:S(2)}, u32[]{:S(2)}) collective-permute-start(bf16[1,192,768]{2,1,0:T(8,128)(2,1)S(1)} %constant_dynamic-slice_fusion.5), channel_id=1, source_target_pairs={{0,2},{1,3},{2,0},{3,1},{4,6},{5,7},{6,4},{7,5},{8,10},{9,11},{10,... | collective-permute-start | bytes 884744 | tf_op jit(solution)/shard_map/ppermute | solution.py:620
  300.5 15.3 %collective-permute-start.8 = (bf16[2,384,384]{2,1,0:T(8,128)(2,1)}, bf16[2,384,384]{2,1,0:T(8,128)(2,1)}, u32[]{:S(2)}, u32[]{:S(2)}) collective-permute-start(bf16[2,384,384]{2,1,0:T(8,128)(2,1)} %dynamic-slice_bitcast_fusion.3), channel_id=1, source_target_pairs={{0,8},{1,9},{2,10},{3,11},{4,12},{5,13},{6,14},{7,15},{8,0},{9,1},... | collective-permute-start | bytes 1769480 | tf_op jit(solution)/shard_map/ppermute | solution.py:620
  301.6 14.7 %collective-permute-start.9 = (bf16[2,384,384]{2,1,0:T(8,128)(2,1)S(1)}, bf16[2,384,384]{2,1,0:T(8,128)(2,1)}, u32[]{:S(2)}, u32[]{:S(2)}) collective-permute-start(bf16[2,384,384]{2,1,0:T(8,128)(2,1)S(1)} %dynamic-slice_bitcast_fusion.2), channel_id=1, source_target_pairs={{0,16},{1,17},{2,18},{3,19},{4,20},{5,21},{6,22},{7,23},{8,24},{9,... | collective-permute-start | bytes 1769480 | tf_op jit(solution)/shard_map/ppermute | solution.py:620
  318.8 10.2 %collective-permute-start.10 = (bf16[384,384]{1,0:T(8,128)(2,1)S(1)}, bf16[384,384]{1,0:T(8,128)(2,1)S(1)}, u32[]{:S(2)}, u32[]{:S(2)}) collective-permute-start(bf16[384,384]{1,0:T(8,128)(2,1)S(1)} %dynamic-slice_bitcast_fusion.9), channel_id=1, source_target_pairs={{0,16},{1,17},{2,18},{3,19},{4,20},{5,21},{6,22},{7,23},{8,24},{9,... | collective-permute-start | bytes 884744 | tf_op jit(solution)/shard_map/ppermute | solution.py:620
  319.9 9.1 %collective-permute-start.11 = (bf16[384,384]{1,0:T(8,128)(2,1)S(1)}, bf16[384,384]{1,0:T(8,128)(2,1)S(1)}, u32[]{:S(2)}, u32[]{:S(2)}) collective-permute-start(bf16[384,384]{1,0:T(8,128)(2,1)S(1)} %dynamic-slice_bitcast_fusion.8), channel_id=1, source_target_pairs={{0,8},{1,9},{2,10},{3,11},{4,12},{5,13},{6,14},{7,15},{8,0},{9,1},... | collective-permute-start | bytes 884744 | tf_op jit(solution)/shard_map/ppermute | solution.py:620
  329.3 8.8 %collective-permute-start.12 = (bf16[2,96,768]{2,1,0:T(8,128)(2,1)S(1)}, bf16[2,96,768]{2,1,0:T(8,128)(2,1)S(1)}, u32[]{:S(2)}, u32[]{:S(2)}) collective-permute-start(bf16[2,96,768]{2,1,0:T(8,128)(2,1)S(1)} %dynamic-slice_bitcast_fusion.7), channel_id=1, source_target_pairs={{0,1},{1,0},{2,3},{3,2},{4,5},{5,4},{6,7},{7,6},{8,9},{9,8},{10,11... | collective-permute-start | bytes 884744 | tf_op jit(solution)/shard_map/ppermute | solution.py:620
  330.2 19.0 %copy-start.3 = (f32[192,768]{1,0:T(8,128)S(1)}, f32[192,768]{1,0:T(8,128)}, u32[]{:S(2)}) copy-start(f32[192,768]{1,0:T(8,128)} %param.20) | copy-start | bytes 1769476
  330.2 19.0 %copy-start.5 = (f32[192,768]{1,0:T(8,128)S(1)}, f32[192,768]{1,0:T(8,128)}, u32[]{:S(2)}) copy-start(f32[192,768]{1,0:T(8,128)} %param.21) | copy-start | bytes 1769476
  330.2 19.0 %copy-start.6 = (f32[192,768]{1,0:T(8,128)S(1)}, f32[192,768]{1,0:T(8,128)}, u32[]{:S(2)}) copy-start(f32[192,768]{1,0:T(8,128)} %param.22) | copy-start | bytes 1769476
  340.0 4.8 %collective-permute-start.14 = (f32[16,13,24]{2,0,1:T(8,128)S(1)}, f32[16,13,24]{2,0,1:T(8,128)S(1)}, u32[]{:S(2)}, u32[]{:S(2)}) collective-permute-start(f32[16,13,24]{2,0,1:T(8,128)S(1)} %dynamic-slice_bitcast_fusion.10), channel_id=1, source_target_pairs={{0,16},{1,17},{2,18},{3,19},{4,20},{5,21},{6,22},{7,23},{8,24},{9,... | collective-permute-start | bytes 59912 | tf_op jit(solution)/shard_map/ppermute | solution.py:620
  344.8 4.2 %collective-permute-start.15 = (f32[8,13,24]{2,0,1:T(8,128)S(1)}, f32[8,13,24]{2,0,1:T(8,128)S(1)}, u32[]{:S(2)}, u32[]{:S(2)}) collective-permute-start(f32[8,13,24]{2,0,1:T(8,128)S(1)} %dynamic-slice_bitcast_fusion.11), channel_id=1, source_target_pairs={{0,8},{1,9},{2,10},{3,11},{4,12},{5,13},{6,14},{7,15},{8,0},{9,1},... | collective-permute-start | bytes 29960 | tf_op jit(solution)/shard_map/ppermute | solution.py:620
  349.0 18.5 %copy-start.4 = (f32[96,768]{1,0:T(8,128)S(1)}, f32[96,768]{1,0:T(8,128)}, u32[]{:S(2)}) copy-start(f32[96,768]{1,0:T(8,128)} %param.17) | copy-start | bytes 884740
  349.1 18.5 %copy-start.10 = (f32[96,768]{1,0:T(8,128)S(1)}, f32[96,768]{1,0:T(8,128)}, u32[]{:S(2)}) copy-start(f32[96,768]{1,0:T(8,128)} %param.18) | copy-start | bytes 884740
  349.1 2.9 collective-permute-start.16
  352.1 5.1 %collective-permute-start.17 = (f32[2,13,24]{2,1,0:T(8,128)S(1)}, f32[2,13,24]{2,1,0:T(8,128)S(1)}, u32[]{:S(2)}, u32[]{:S(2)}) collective-permute-start(f32[2,13,24]{2,1,0:T(8,128)S(1)} %bitcast.130), channel_id=1, source_target_pairs={{0,2},{1,3},{2,0},{3,1},{4,6},{5,7},{6,4},{7,5},{8,10},{9,11},{10,... | collective-permute-start | bytes 7496 | tf_op jit(solution)/shard_map/ppermute | solution.py:620
  357.1 3.7 collective-permute-start.18
  358.8 8.8 %collective-permute-start.13 = (bf16[1,96,768]{2,1,0:T(8,128)(2,1)S(1)}, bf16[1,96,768]{2,1,0:T(8,128)(2,1)S(1)}, u32[]{:S(2)}, u32[]{:S(2)}) collective-permute-start(bf16[1,96,768]{2,1,0:T(8,128)(2,1)S(1)} %constant_dynamic-slice_fusion.4), channel_id=1, source_target_pairs={{0,2},{1,3},{2,0},{3,1},{4,6},{5,7},{6,4},{7,5},{8,10},{9,11},{10,... | collective-permute-start | bytes 442376 | tf_op jit(solution)/shard_map/ppermute | solution.py:620
  (10 other events, 82.9 us)

commit v2 on v1

--- a/solution.py
+++ b/solution.py
@@ -291,7 +291,7 @@
     att = Spreading(wide, narrow, att_ref, w_ref, pairs, sems[:count])
     ff = Spreading(wide, narrow, ff_ref, fout_ref, pairs, sems[count:2 * count])
     vs = Spreading(wide, narrow, vs_ref, vs_scr, [(0, 128, False)], sems[2 * count:])
-    singles = [r for r in range(1, wide // 2)]
+    levels = {deep: [r for r in range(1, wide // 2) if (r & (r - 1) != 0) == deep] for deep in (False, True)}
     save = pltpu.make_async_copy(w_ref, wout_ref, put_sem)
 
     @pl.when(i == 0)
@@ -303,7 +303,7 @@
             vs.roots(k)
             att.roots(k)
         ff.roots(0)
-        for r in singles:
+        for r in range(1, wide // 2):
             for k in range(narrow):
                 vs.relay(r, k)
                 att.relay(r, k)
@@ -318,9 +318,9 @@
         att.close()
         save.start()
 
-    plan = [lambda k=k: ff.roots(k) for k in range(1, narrow)]
-    for r in singles:
-        plan += [lambda r=r, k=k: ff.relay(r, k) for k in range(narrow)]
+    plan = [[lambda k=k: ff.roots(k)] for k in range(1, narrow)]
+    for r in range(1, wide // 2):
+        plan += [[lambda r=r, k=k: ff.relay(r, k)] for k in range(narrow)]
 
     def service(point):
         for s in range(steps):
@@ -332,9 +332,9 @@
                         act()
     total = steps * 3 - 1
     slots = {}
-    for n, act in enumerate(plan):
+    for n, group in enumerate(plan):
         spot = n * total // len(plan)
-        slots.setdefault((spot // 3, spot % 3), []).append(act)
+        slots.setdefault((spot // 3, spot % 3), []).extend(group)
 
     attend_forward(i, tok_ref, seg_ref, feat_ref, w_ref, vec_ref, mixed_ref, q_ref, k_ref, v_ref, ctx_ref, lse_ref, bias_scr, service)
 
@@ -366,6 +366,88 @@
         cost_estimate=cost(60, 60),
         name="gather_attend",
     )(tokens, seg, feat, att_shard, ff_shard, vs)
+
+def masks_of(bits):
+    found = [0]
+    for b in bits:
+        found = found + [m | b for m in found]
+    return sorted(found, key=lambda m: (-bin(m).count("1"), m))
+
+
+class Halving:
+    def __init__(self, wide, narrow, total, tree_refs, line_refs, sems):
+        bits = [1 << b for b in range((wide // 2).bit_length() - 1)]
+        w, self.z = lax.axis_index("wide"), lax.axis_index("narrow")
+        self.o, self.c = w // 2, w % 2
+        self.total, self.tree_refs, self.line_refs, self.sems = total, tree_refs, line_refs, sems
+        self.rows = total.shape[1] // narrow
+        self.orders = [bits, bits[::-1]]
+        self.line_bits = [1 << b for b in range(narrow.bit_length() - 1)]
+        self.names = [("tree", h, t, m) for t in range(len(bits)) for h in range(2) for m in masks_of(self.orders[h][t + 1:])]
+        if line_refs:
+            self.names += [("line", 0, t, m) for t in range(len(self.line_bits)) for m in masks_of(self.line_bits[t + 1:])]
+
+    def copy(self, name):
+        kind, h, t, m = name
+        n = self.names.index(name)
+        if kind == "tree":
+            bit = self.orders[h][t]
+            cols = pl.ds(h * (D // 2), D // 2)
+            slot = masks_of(self.orders[h][t + 1:]).index(m)
+            source = self.total.at[flips(self.o, bit | m), :, cols]
+            landing = self.tree_refs[t].at[h, slot]
+            device = (2 * flips(self.o, bit) + self.c, self.z)
+        else:
+            bit = self.line_bits[t]
+            slot = masks_of(self.line_bits[t + 1:]).index(m)
+            source = self.total.at[self.o, pl.ds(pl.multiple_of(flips(self.z, bit | m) * self.rows, 8), self.rows), :]
+            landing = self.line_refs[t].at[slot]
+            device = (2 * self.o + self.c, flips(self.z, bit))
+        return pltpu.make_async_remote_copy(source, landing, self.sems[0].at[n], self.sems[1].at[n], device_id=device, device_id_type=MESH)
+
+    def pick(self, kind, turn, deep):
+        return [n for n in self.names if n[0] == kind and n[2] == turn and (n[3] != 0) == deep]
+
+    def send(self, kind, turn):
+        for deep in (True, False):
+            for name in self.pick(kind, turn, deep):
+                self.copy(name).start()
+
+    def take(self, kind, turn, deep):
+        for name in self.pick(kind, turn, deep):
+            self.copy(name).wait_recv()
+            _, h, t, m = name
+            if kind == "tree":
+                cols = pl.ds(h * (D // 2), D // 2)
+                slot = masks_of(self.orders[h][t + 1:]).index(m)
+                self.total[flips(self.o, m), :, cols] = self.total[flips(self.o, m), :, cols] + self.tree_refs[t][h, slot]
+            else:
+                slot = masks_of(self.line_bits[t + 1:]).index(m)
+                at = pl.ds(pl.multiple_of(flips(self.z, m) * self.rows, 8), self.rows)
+                self.total[self.o, at, :] = self.total[self.o, at, :] + self.line_refs[t][slot]
+
+    def drain(self):
+        for name in self.names:
+            self.copy(name).wait_send()
+
+
+def halving_scratch(wide, narrow, rows, line):
+    outer, inner = (wide // 2).bit_length() - 1, narrow.bit_length() - 1
+    groups = wide // 2
+    shapes = [VMEM((groups, narrow * rows, D), BF16)]
+    shapes += [VMEM((2, groups >> (t + 1), narrow * rows, D // 2), BF16) for t in range(outer)]
+    count = 2 * (groups - 1)
+    if line:
+        shapes += [VMEM((narrow >> (t + 1), rows, D), BF16) for t in range(inner)]
+        count += narrow - 1
+    return shapes + [pltpu.SemaphoreType.DMA((count,)), pltpu.SemaphoreType.DMA((count,))]
+
+
+def begin_total(total, mine_ref, got_ref):
+    def one(g, carry):
+        total[g] = mine_ref[g] + got_ref[g]
+        return carry
+    lax.fori_loop(0, total.shape[0], one, 0)
 
 def norm_parts(z):
     mean = jnp.mean(z, axis=1, keepdims=True)
@@ -482,13 +564,10 @@
         name="weight_grad",
     )(side, lhs, rhs)
 
-def k3_body(first_seq, kept, q_ref, k_ref, v_ref, ctx_ref, dctx_ref, fb_ref, lse_ref, seg_ref, *rest):
-    d_ref, vg_ref, bias_scr, lse_scr, del_scr = rest[kept:]
+def attend_back_step(i, q_ref, k_ref, v_ref, ctx_ref, dctx_ref, fb_ref, lse_ref, seg_ref, d_ref, vg_ref, bias_scr, lse_scr, del_scr, service):
     ctx_ref = ctx_ref.at[0]
     dq_ref, dk_ref, dv_ref = d_ref.at[0], d_ref.at[1], d_ref.at[2]
     d_ref[3] = fb_ref[...]
-    i = pl.program_id(0) + first_seq
-
     @pl.when(pl.program_id(0) == 0)
     def _():
         vg_ref[...] = jnp.zeros_like(vg_ref)
@@ -526,7 +605,16 @@
         vg_ref[0:1, at] += colsum(dqb.astype(F32))
         vg_ref[1:2, at] += colsum(dvb.astype(F32))
         return carry
-    lax.fori_loop(0, HEADS // 2, pair, 0)
+    service(0)
+    lax.fori_loop(0, HEADS // 4, pair, 0)
+    service(1)
+    lax.fori_loop(HEADS // 4, HEADS // 2, pair, 0)
+    service(2)
+
+
+def k3_body(first_seq, kept, *refs):
+    ins, rest = refs[:8], refs[8 + kept:]
+    attend_back_step(pl.program_id(0) + first_seq, *ins, *rest, lambda point: None)
 
 
 def k3(first_seq, count, q, k, v, ctx, dctx, fb, lse, seg, kept):
@@ -546,9 +634,61 @@
         name="attend_back",
     )(q, k, v, ctx, dctx, fb, lse, seg, *kept)
 
-def k4_body(first_seq, kept, first_ref, d_ref, tok_ref, seg_ref, feat_ref, w_ref, vec_ref, *rest):
-    tg_ref, vg_ref = rest[kept:]
-    i = pl.program_id(0) + first_seq
+def summing_k3_body(wide, narrow, steps, *refs):
+    ins, (mine_ref, got_ref, d_ref, vg_ref, own_ref), rest = refs[:8], refs[8:13], refs[13:]
+    (bias_scr, lse_scr, del_scr, total), rest = rest[:4], rest[4:]
+    *tree_refs, out_sems, in_sems = rest
+    i = pl.program_id(0)
+    turns = len(tree_refs)
+    half = Halving(wide, narrow, total, tree_refs, [], (out_sems, in_sems))
+
+    @pl.when(i == 0)
+    def _():
+        greet(wide, 1)
+        begin_total(total, mine_ref, got_ref)
+        half.send("tree", 0)
+
+    def service(point):
+        for t in range(turns):
+            spot = 3 * steps * (t + 1) // (turns + 1) - 1 if t < turns - 1 else 3 * steps - 2
+            if spot % 3 == point:
+                @pl.when(i == spot // 3)
+                def _(t=t):
+                    if t < turns - 1:
+                        half.take("tree", t, True)
+                        half.send("tree", t + 1)
+                    else:
+                        for done in range(turns):
+                            half.take("tree", done, False)
+
+    attend_back_step(i, *ins, d_ref, vg_ref, bias_scr, lse_scr, del_scr, service)
+
+    @pl.when(i == steps - 1)
+    def _():
+        half.drain()
+        own_ref[...] = total[lax.axis_index("wide") // 2]
+
+
+def summing_k3(wide, narrow, q, k, v, ctx, dctx, fb, lse, seg, mine, got):
+    seqs, length = seg.shape
+    n = seqs * length
+    blk = pl.BlockSpec((length, D), lambda i: (i, 0))
+    span = mine.shape[1]
+    return pl.pallas_call(
+        partial(summing_k3_body, wide, narrow, seqs), grid=(seqs,),
+        in_specs=[blk] * 3 + [pl.BlockSpec((1, length, D), lambda i: (1, i, 0)), blk, blk,
+                              pl.BlockSpec((length, 128), lambda i: (i, 0)), whole((seqs, length)), whole(mine.shape), whole(got.shape)],
+        out_specs=[pl.BlockSpec((4, length, D), lambda i: (0, i, 0)), whole((8, D)), whole((span, D))],
+        out_shape=[jax.ShapeDtypeStruct((4, n, D), BF16), jax.ShapeDtypeStruct((8, D), F32), jax.ShapeDtypeStruct((span, D), BF16)],
+        scratch_shapes=[VMEM((length, length), F32), VMEM((16, length), F32), VMEM((16, length), F32),
+                        *halving_scratch(wide, narrow, span // narrow, False)],
+        compiler_params=pltpu.CompilerParams(collective_id=1, has_side_effects=True),
+        cost_estimate=cost(60, 40),
+        name="attend_back_sum",
+    )(q, k, v, ctx, dctx, fb, lse, seg, mine, got)
+
+
+def token_back_step(i, first_ref, d_ref, tok_ref, seg_ref, feat_ref, w_ref, vec_ref, tg_ref, vg_ref):
     dq_ref, dk_ref, dv_ref = d_ref.at[0], d_ref.at[1], d_ref.at[2]
 
     @pl.when(pl.program_id(0) == 0)
@@ -565,6 +705,99 @@
     vg_ref[0:1, :] += colsum(mg * merging)
     spread = (vec_ref[0:1, :] * mg / members).astype(BF16)
     tg_ref[...] = (mg + nn(gb, spread)).astype(BF16)
+
+
+def k4_body(first_seq, kept, *refs):
+    token_back_step(pl.program_id(0) + first_seq, *refs[:7], *refs[7 + kept:])
+
+
+def summing_k4_body(wide, narrow, steps, *refs):
+    ins, (mine_ref, got_ref, vg2_ref, vg3_ref, tg_ref, own_ref, vec_out), rest = refs[:7], refs[7:14], refs[14:]
+    (vg_scr, total), rest = rest[:2], rest[2:]
+    outer, inner = (wide // 2).bit_length() - 1, narrow.bit_length() - 1
+    tree_refs, line_refs, rest = rest[:outer], rest[outer:outer + inner], rest[outer + inner:]
+    out_sems, in_sems, sum_scr, came_scr, vec_sems_out, vec_sems_in = rest
+    i = pl.program_id(0)
+    half = Halving(wide, narrow, total, tree_refs, line_refs, (out_sems, in_sems))
+    w, z = lax.axis_index("wide"), lax.axis_index("narrow")
+    o, c = w // 2, w % 2
+    peers = [(2 * o + 1 - c, z)] + [(2 * flips(o, 1 << b) + c, z) for b in range(outer)] + [(w, flips(z, 1 << b)) for b in range(inner)]
+
+    def across(n):
+        return pltpu.make_async_remote_copy(sum_scr.at[n], came_scr.at[n], vec_sems_out.at[n], vec_sems_in.at[n],
+                                            device_id=peers[n], device_id_type=MESH)
+
+    @pl.when(i == 0)
+    def _():
+        greet(wide, narrow)
+        begin_total(total, mine_ref, got_ref)
+        half.send("tree", 0)
+
+    token_back_step(i, *ins, tg_ref, vg_scr)
+
+    for t in range(outer - 1):
+        @pl.when(i == min(steps - 1, (steps * (t + 1)) // (outer + 1)))
+        def _(t=t):
+            half.take("tree", t, True)
+            half.send("tree", t + 1)
+
+    @pl.when(i == steps - 1)
+    def _():
+        sum_scr[0, 0:1, :] = vg_scr[0:1, :]
+        sum_scr[0, 1:3, :] = vg3_ref[0:2, :]
+        sum_scr[0, 3:13, :] = vg2_ref[0:10, :]
+        sum_scr[0, 13:16, :] = jnp.zeros((3, D), F32)
+        across(0).start()
+        for t in range(outer):
+            half.take("tree", t, False)
+        half.send("line", 0)
+        turn = 0
+        for n in range(len(peers)):
+            across(n).wait_recv()
+            added = sum_scr[n] + came_scr[n]
+            if n + 1 < len(peers):
+                sum_scr[n + 1] = added
+                across(n + 1).start()
+            else:
+                vec_out[...] = added
+            if n % 2 == 1 and turn < inner - 1:
+                half.take("line", turn, True)
+                half.take("line", turn, False)
+                turn += 1
+                half.send("line", turn)
+        while turn < inner - 1:
+            half.take("line", turn, True)
+            half.take("line", turn, False)
+            turn += 1
+            half.send("line", turn)
+        last = half.pick("line", turn, False)[0]
+        half.copy(last).wait_recv()
+        at = pl.ds(pl.multiple_of(z * half.rows, 8), half.rows)
+        own_ref[...] = total[o, at, :].astype(F32) + line_refs[turn][0].astype(F32)
+        half.drain()
+        for n in range(len(peers)):
+            across(n).wait_send()
+
+
+def summing_k4(wide, narrow, first, d, tokens, seg, feat, att, vec, mine, got, vg2, vg3):
+    seqs, length = seg.shape
+    n = seqs * length
+    blk = pl.BlockSpec((length, D), lambda i: (i, 0))
+    rows = mine.shape[1] // narrow
+    stages = (wide * narrow).bit_length() - 1
+    return pl.pallas_call(
+        partial(summing_k4_body, wide, narrow, seqs), grid=(seqs,),
+        in_specs=[blk, pl.BlockSpec((3, length, D), lambda i: (0, i, 0)), blk, whole(seg.shape), whole(feat.shape),
+                  pl.BlockSpec((3 * D, D), lambda i: (0, 0), pipeline_mode=pl.Buffered(1)), whole(vec.shape),
+                  whole(mine.shape), whole(got.shape), whole(vg2.shape), whole(vg3.shape)],
+        out_specs=[blk, whole((rows, D)), whole((16, D))],
+        out_shape=[jax.ShapeDtypeStruct((n, D), BF16), jax.ShapeDtypeStruct((rows, D), F32), jax.ShapeDtypeStruct((16, D), F32)],
+        scratch_shapes=[VMEM((8, D), F32), *halving_scratch(wide, narrow, rows, True),
+                        VMEM((stages, 16, D), F32), VMEM((stages, 16, D), F32), pltpu.SemaphoreType.DMA((stages,)), pltpu.SemaphoreType.DMA((stages,))],
+        compiler_params=pltpu.CompilerParams(collective_id=2, has_side_effects=True),
+        cost_estimate=cost(30, 30),
+        name="token_grad_sum",
+    )(first, d, tokens, seg, feat, att, vec, mine, got, vg2, vg3)
 
 
 def k4(first_seq, count, first, d, tokens, seg, feat, att, vec, kept):
@@ -682,6 +915,11 @@
         self.values = [h.reshape((2,) * width + h.shape[1:]) for h in (total[:, :, :D // 2], total[:, :, D // 2:])]
         self.split()
 
+    def resume(self, own):
+        self.done = len(self.orders[0])
+        self.values = [own]
+        self.split()
+
     def split(self):
         turn, outer = self.done, len(self.orders[0])
         if turn < outer:
@@ -725,6 +963,12 @@
         grad = add(part(both, me, bit, 0, True), swap(part(both, me, bit, 0, False), bit, devices), F32)
         bit //= 2
     return grad[0]
+
+
+def one_side(me, lhs, rhs, wide, narrow, owned, mine):
+    side = (me // narrow) % 2
+    side = side if mine else 1 - side
+    return dw(side.reshape(1).astype(jnp.int32), lhs, rhs, narrow * owned, wide // 2)
 
 
 def split_grads(me, lhs, rhs, wide, narrow, owned):
@@ -798,6 +1042,44 @@
     return (*held, vec, natural, ff, offsets)
 
 
+def backward_by_permutes(me, wide, narrow, tokens, seg, feat, held, out_parts, natural, vec, owned):
+    devices, seqs = wide * narrow, seg.shape[0]
+    q, k, v, ctx, lse = held
+    first, fb, dctx, broad, slim, vg2 = out_parts
+    ff_sum = Scatter(me, wide, narrow)
+    ff_sum.begin(*split_grads(me, broad, slim, wide, narrow, owned[0]))
+    vg3, held, ff_owned = 0.0, (), None
+    for first_seq, count in spread(seqs, (2, 1, 1)):
+        def attend(given):
+            source, kept = given
+            return k3(first_seq, count, *source, ctx, dctx, fb, lse, seg, kept)
+        (grads, more), ff_owned = ff_sum.over(((q, k, v), held), attend)
+        held, vg3 = (grads,), vg3 + more
+    d = held[0]
+    if ff_owned is None:
+        (mine, got), ff_owned = ff_sum.over((ctx, d), lambda g: split_grads(me, *g, wide, narrow, owned[1]))
+    else:
+        mine, got = split_grads(me, ctx, d, wide, narrow, owned[1])
+    while ff_owned is None:
+        _, ff_owned = ff_sum.over((), lambda g: ())
+    att_sum = Scatter(me, wide, narrow)
+    att_sum.begin(mine, got)
+    vg4, held, att_owned = 0.0, (), None
+    for first_seq, count in spread(seqs, (2, 1, 1)):
+        def back(given):
+            source, kept = given
+            return k4(first_seq, count, source, d, tokens, seg, feat, natural, vec, kept)
+        (grads, more), att_owned = att_sum.over((first, held), back)
+        held, vg4 = (grads,), vg4 + more
+    token_grads = held[0]
+    vec_grad = jnp.concatenate([vg4[0:1], vg3[0:2], vg2[:10]], axis=0)
+    vec_owned = scatter_small(jnp.transpose(vec_grad.reshape(vec_grad.shape[0], devices, -1), (1, 0, 2)), me, wide, narrow)
+    while att_owned is None:
+        att_sum.turn()
+        att_owned = att_sum.take()
+    return token_grads, ff_owned, att_owned, vec_owned
+
+
 def local(wide, narrow, tokens, cotangent, segment_ids, feature_ids,
           attention_master, attention_first, attention_second,
           feedforward_master, feedforward_first, feedforward_second,
@@ -815,37 +1097,28 @@
         *held, vec, natural, ff, offsets = forward_by_permutes(me, wide, narrow, tokens, seg, feat, *shards)
     mixed, q, k, v, ctx, lse = held
     out, first, fb, dctx, broad, slim, vg2 = k2(me1, mixed, ctx, cotangent, natural, ff, offsets, vec)
-    ff_sum = Scatter(me, wide, narrow)
-    ff_sum.begin(*split_grads(me, broad, slim, wide, narrow, feedforward_master.shape[0]))
-    vg3, held, ff_owned = 0.0, (), None
-    for first_seq, count in spread(seqs, (2, 1, 1)):
-        def attend(given):
-            source, kept = given
-            return k3(first_seq, count, *source, ctx, dctx, fb, lse, seg, kept)
-        (grads, more), ff_owned = ff_sum.over(((q, k, v), held), attend)
-        held, vg3 = (grads,), vg3 + more
-    d = held[0]
-    if ff_owned is None:
-        (mine, got), ff_owned = ff_sum.over((ctx, d), lambda g: split_grads(me, *g, wide, narrow, attention_master.shape[0]))
+    parts = (first, fb, dctx, broad, slim, vg2)
+    rows = (feedforward_master.shape[0], attention_master.shape[0])
+    if devices <= 32:
+        mine, got = split_grads(me, broad, slim, wide, narrow, rows[0])
+        d, vg3, own = summing_k3(wide, narrow, q, k, v, ctx, dctx, fb, lse, seg, mine, got)
+        ff_sum = Scatter(me, wide, narrow)
+        ff_sum.resume(own)
+        lhs, ff_owned = ctx, None
+        sent, ff_owned = ff_sum.over((lhs, d), lambda g: one_side(me, *g, wide, narrow, rows[1], False))
+        back = swap(sent, narrow, devices)
+        if ff_owned is None:
+            mine, ff_owned = ff_sum.over((lhs, d), lambda g: one_side(me, *g, wide, narrow, rows[1], True))
+        else:
+            mine = one_side(me, lhs, d, wide, narrow, rows[1], True)
+        while ff_owned is None:
+            _, ff_owned = ff_sum.over((), lambda g: ())
+        token_grads, att_owned, vec_sum = summing_k4(wide, narrow, first, d, tokens, seg, feat, natural, vec, mine, back, vg2, vg3)
+        width = vector_master.shape[1]
+        vec_owned = lax.dynamic_slice(vec_sum, (0, me * width), (vector_master.shape[0], width))
     else:
-        mine, got = split_grads(me, ctx, d, wide, narrow, attention_master.shape[0])
-    while ff_owned is None:
-        _, ff_owned = ff_sum.over((), lambda g: ())
-    att_sum = Scatter(me, wide, narrow)
-    att_sum.begin(mine, got)
-    vg4, held, att_owned = 0.0, (), None
-    for first_seq, count in spread(seqs, (2, 1, 1)):
-        def back(given):
-            source, kept = given
-            return k4(first_seq, count, source, d, tokens, seg, feat, natural, vec, kept)
-        (grads, more), att_owned = att_sum.over((first, held), back)
-        held, vg4 = (grads,), vg4 + more
-    token_grads = held[0]
-    vec_grad = jnp.concatenate([vg4[0:1], vg3[0:2], vg2[:10]], axis=0)
-    vec_owned = scatter_small(jnp.transpose(vec_grad.reshape(vec_grad.shape[0], devices, -1), (1, 0, 2)), me, wide, narrow)
-    while att_owned is None:
-        att_sum.turn()
-        att_owned = att_sum.take()
+        token_grads, ff_owned, att_owned, vec_owned = backward_by_permutes(
+            me, wide, narrow, tokens, seg, feat, (q, k, v, ctx, lse), parts, natural, vec, rows)
     ff_rate = rates(feedforward_master.shape[0], FF, D ** (-0.5), FF ** (-0.5))
     att_rate = rates(attention_master.shape[0], 3 * D, D ** (-0.5), (D // 64) ** (-0.5))
     f_new = adam_step(feedforward_master, feedforward_first, feedforward_second, ff_owned, ff_rate)

time: 375 us -> 340 us (0.907); the launches traced: 369 us -> 339 us
  Pallas kernels: 294 us -> 313 us
  other arithmetic: 26.4 us -> 9.51 us
  starting transfers between devices: 18 us -> 1.57 us
  waiting for transfers between devices: 24 us -> 8.37 us
    pallas_call x6 -> x2, Pallas kernels: 81.9 us -> 102 us  [the longest x1 56.4 us: summing_k3(): pl.pallas_call(partial(summing_k3_body, wide, narrow, seqs), grid=(seqs,)...]
    ppermute x19 -> x4, starting transfers between devices: 18 us -> 1.57 us  [swap(): return lax.ppermute(value, BOTH, [(i, i ^ bit) for i in range(devices)])]
    ppermute x19 -> x4, waiting for transfers between devices: 24 us -> 8.37 us  [swap(): return lax.ppermute(value, BOTH, [(i, i ^ bit) for i in range(devices)])]
    convert_element_type x11 -> x1, other arithmetic: 15 us -> 0.15 us  [add(): return (a.astype(F32) + b.astype(F32)).astype(kind)]
  transfers between devices with their start and end apart: 19 -> 4, of which waited for: 10 -> 2; matrix products, arithmetic and copies ran while one was open for 1% -> 1% of each run, Pallas kernels for 29% -> 11%
where the time goes in v2:
time: 340 us; the launch traced here: 339 us
  Pallas kernels  313 us (92%)
  other arithmetic  9.51 us (3%)
  waiting for transfers between devices  8.37 us (2%)
  local copies, waits for them, and re-layouts  5.56 us (2%)
    pallas_call x1, Pallas kernels, gathering_k1(): pl.pallas_call(partial(gathering_k1_body, wide, narrow, vec_shard.shape[1...  92.2 us
    pallas_call x1, Pallas kernels, k2(): pl.pallas_call(partial(k2_body, offsets), grid_spec=pltpu.PrefetchScalarG...  68.2 us
    pallas_call x1, Pallas kernels, summing_k3(): pl.pallas_call(partial(summing_k3_body, wide, narrow, seqs), grid=(seqs,)...  56.4 us
    pallas_call x4, Pallas kernels, dw(): pl.pallas_call(partial(dw_body, rows), grid_spec=pltpu.PrefetchScalarGrid...  50.8 us
    pallas_call x1, Pallas kernels, summing_k4(): pl.pallas_call(partial(summing_k4_body, wide, narrow, seqs), grid=(seqs,)...  45.7 us
    ppermute x4, waiting for transfers between devices, swap(): return lax.ppermute(value, BOTH, [(i, i ^ bit) for i in range(devices)])  8.37 us
  transfers between devices with their start and end apart: 4, of which 2 were waited for; matrix products, arithmetic and copies ran while one was open for 1% of the time, Pallas kernels for 11%

profile of v2, /device:TPU:0, one launch (start us, length us, event | category | flops | bytes accessed | tf_op | source)
XLA Modules:
  0.0 339.2 jit_solution(16378010386811479540)
XLA Ops:
  0.7 1.6 convert_element_type.48.att_ref
  2.3 1.8 convert_element_type.49.ff_ref
  4.1 0.7 convert_element_type.50
  4.8 0.6 pad.4.vs_ref
  5.4 92.2 %gather_attend.1 = (f32[2048,768]{1,0:T(8,128)}, bf16[2048,768]{1,0:T(8,128)(2,1)}, bf16[2048,768]{1,0:T(8,128)(2,1)}, bf16[2048,768]{1,0:T(8,128)(2,1)}, bf16[2...) custom-call(bf16[2048,768]{1,0:T(8,128)(2,1)} %refs_2_.1, ...), custom_call_target="tpu_custom_call" | custom-call | flops 60000002048 | bytes 60000000 | tf_op jit(solution)/shard_map/gather_attend/pallas_call | solution.py:357
  97.7 68.2 %feed_forward.1 = (bf16[2048,768]{1,0:T(8,128)(2,1)}, f32[2048,768]{1,0:T(8,128)}, bf16[2048,768]{1,0:T(8,128)(2,1)}, bf16[2048,768]{1,0:T(8,128)(2,1)}, bf16[2,...) custom-call(s32[1]{0:T(128)} %bitcast.self_ref, ...), custom_call_target="tpu_custom_call" | custom-call | flops 60000002048 | bytes 80000000 | tf_op jit(solution)/shard_map/feed_forward/pallas_call | solution.py:525
  165.9 15.1 %weight_grad.4 = bf16[4,768,768]{2,1,0:T(8,128)(2,1)} custom-call(s32[1]{0:T(128)} %bitcast.2.side_ref, bf16[2,2048,3072]{2,1,0:T(8,128)(2,1)} %get-tuple-element.63.lhs_ref, bf16[2,2048,768]{2,1,0:T(8,128)(2,1)} %get-tuple-element.62.rhs_ref), custom_call_target="tpu_custom_call" | custom-call | flops 9663676416 | bytes 10000000 | tf_op jit(solution)/shard_map/weight_grad/pallas_call | solution.py:554
  181.0 0.4 collective-permute-start
  181.4 15.1 %weight_grad.5.refs_8_ = bf16[4,768,768]{2,1,0:T(8,128)(2,1)} custom-call(s32[1]{0:T(128)} %bitcast.1.side_ref, bf16[2,2048,3072]{2,1,0:T(8,128)(2,1)} %get-tuple-element.63.lhs_ref, bf16[2,2048,768]{2,1,0:T(8,128)(2,1)} %get-tuple-element.62.rhs_ref), custom_call_target="tpu_custom_call" | custom-call | flops 9663676416 | bytes 10000000 | tf_op jit(solution)/shard_map/weight_grad/pallas_call | solution.py:554
  196.5 56.4 %attend_back_sum.1 = (bf16[4,2048,768]{2,1,0:T(8,128)(2,1)}, f32[8,768]{1,0:T(8,128)}, bf16[768,768]{1,0:T(8,128)(2,1)}) custom-call(bf16[2048,768]{1,0:T(8,128)(2,1)} %get-tuple-element.55.refs_0_, bf16[2048,768]{1,0:T(8,128)(2,1)} %get-tuple-element.56.refs_1_, bf16[2048,768]{1,0:T(8,128)(2,1)} %get-tuple-element.57.refs_2_, ...), custom_call_target="tpu_custom_call" | custom-call | flops 60000002048 | bytes 40000000 | tf_op jit(solution)/shard_map/attend_back_sum/pallas_call | solution.py:677
  252.8 1.1 dynamic-slice_bitcast_fusion
  254.0 0.2 collective-permute-start.1
  254.1 10.4 %weight_grad.6 = bf16[4,384,768]{2,1,0:T(8,128)(2,1)} custom-call(s32[1]{0:T(128)} %bitcast.2.side_ref, bf16[2,2048,768]{2,1,0:T(8,128)(2,1)} %get-tuple-element.72.ctx_ref.refs_3_.lhs_ref, bf16[4,2048,768]{2,1,0:T(8,128)(2,1)} %get-tuple-element.73.rhs_ref.refs_1_), custom_call_target="tpu_custom_call" | custom-call | flops 4831838208 | bytes 10000000 | tf_op jit(solution)/shard_map/weight_grad/pallas_call | solution.py:554
  264.5 3.2 collective-permute-done.1
  267.8 0.2 fusion
  268.0 0.0 copy-start.3
  268.0 1.0 collective-permute-start.2
  269.0 10.3 %weight_grad.7.refs_7_ = bf16[4,384,768]{2,1,0:T(8,128)(2,1)} custom-call(s32[1]{0:T(128)} %bitcast.1.side_ref, bf16[2,2048,768]{2,1,0:T(8,128)(2,1)} %get-tuple-element.72.ctx_ref.refs_3_.lhs_ref, bf16[4,2048,768]{2,1,0:T(8,128)(2,1)} %get-tuple-element.73.rhs_ref.refs_1_), custom_call_target="tpu_custom_call" | custom-call | flops 4831838208 | bytes 10000000 | tf_op jit(solution)/shard_map/weight_grad/pallas_call | solution.py:554
  279.3 5.1 %collective-permute-done.2 = bf16[1,192,768]{2,1,0:T(8,128)(2,1)S(1)} collective-permute-done((bf16[1,192,768]{2,1,0:T(8,128)(2,1)S(1)}, bf16[1,192,768]{2,1,0:T(8,128)(2,1)S(1)}, u32[]{:S(2)}, u32[]{:S(2)}) %collective-permute-start.2) | collective-permute-done | bytes 294944 | tf_op jit(solution)/shard_map/ppermute | solution.py:853
  284.4 1.7 fusion.6
  286.2 45.7 %token_grad_sum.1 = (bf16[2048,768]{1,0:T(8,128)(2,1)}, f32[96,768]{1,0:T(8,128)}, f32[16,768]{1,0:T(8,128)}) custom-call(f32[2048,768]{1,0:T(8,128)} %get-tuple-element.54.refs_0_, bf16[4,2048,768]{2,1,0:T(8,128)(2,1)} %get-tuple-element.73.rhs_ref.refs_1_, bf16[2048,768]{1,0:T(8,128)(2,1)} %refs_2_.1, s32[4,512]{1,0:T(4,128)} %refs_3_.1, ...), custom_call_target="tpu_custom_call" | custom-call | flops 30000001024 | bytes 30000000 | tf_op jit(solution)/shard_map/token_grad_sum/pallas_call | solution.py:788
  332.0 2.1 fusion.8
  334.1 1.4 fusion.4
  335.5 3.8 %copy.30 = bf16[2048,768]{1,0:T(8,128)(2,1)} copy(bf16[2048,768]{1,0:T(8,128)(2,1)} %get-tuple-element.109) | data formatting | bytes 6291456
  (25 shorter events, 0.1 us)
Async XLA Ops:
  181.0 15.5 %collective-permute-start = (bf16[4,768,768]{2,1,0:T(8,128)(2,1)}, bf16[4,768,768]{2,1,0:T(8,128)(2,1)}, u32[]{:S(2)}, u32[]{:S(2)}) collective-permute-start(bf16[4,768,768]{2,1,0:T(8,128)(2,1)} %weight_grad.4), channel_id=1, source_target_pairs={{0,4},{1,5},{2,6},{3,7},{4,0},{5,1},{6,2},{7,3},{8,12},{9,13},{10,... | collective-permute-start | bytes 14155784 | tf_op jit(solution)/shard_map/ppermute | solution.py:853
  254.0 13.8 %copy-start.2 = (bf16[768,768]{1,0:T(8,128)(2,1)S(1)}, bf16[768,768]{1,0:T(8,128)(2,1)}, u32[]{:S(2)}) copy-start(bf16[768,768]{1,0:T(8,128)(2,1)} %get-tuple-element.66) | copy-start | bytes 3538948
  254.0 13.8 %collective-permute-start.1 = (bf16[2,192,768]{2,1,0:T(8,128)(2,1)S(1)}, bf16[2,192,768]{2,1,0:T(8,128)(2,1)S(1)}, u32[]{:S(2)}, u32[]{:S(2)}) collective-permute-start(bf16[2,192,768]{2,1,0:T(8,128)(2,1)S(1)} %dynamic-slice_bitcast_fusion), channel_id=1, source_target_pairs={{0,1},{1,0},{2,3},{3,2},{4,5},{5,4},{6,7},{7,6},{8,9},{9,8},{10,11... | collective-permute-start | bytes 1769480 | tf_op jit(solution)/shard_map/ppermute | solution.py:853
  267.7 18.4 %collective-permute-start.3 = (bf16[4,384,768]{2,1,0:T(8,128)(2,1)}, bf16[4,384,768]{2,1,0:T(8,128)(2,1)}, u32[]{:S(2)}, u32[]{:S(2)}) collective-permute-start(bf16[4,384,768]{2,1,0:T(8,128)(2,1)} %weight_grad.6), channel_id=1, source_target_pairs={{0,4},{1,5},{2,6},{3,7},{4,0},{5,1},{6,2},{7,3},{8,12},{9,13},{10,... | collective-permute-start | bytes 7077896 | tf_op jit(solution)/shard_map/ppermute | solution.py:853
  268.0 16.5 %copy-start = (f32[192,768]{1,0:T(8,128)S(1)}, f32[192,768]{1,0:T(8,128)}, u32[]{:S(2)}) copy-start(f32[192,768]{1,0:T(8,128)} %param.20) | copy-start | bytes 1769476
  268.0 16.5 %copy-start.3 = (f32[192,768]{1,0:T(8,128)S(1)}, f32[192,768]{1,0:T(8,128)}, u32[]{:S(2)}) copy-start(f32[192,768]{1,0:T(8,128)} %param.21) | copy-start | bytes 1769476
  268.0 16.4 %copy-start.4 = (f32[192,768]{1,0:T(8,128)S(1)}, f32[192,768]{1,0:T(8,128)}, u32[]{:S(2)}) copy-start(f32[192,768]{1,0:T(8,128)} %param.22) | copy-start | bytes 1769476
  268.0 16.4 %collective-permute-start.2 = (bf16[1,192,768]{2,1,0:T(8,128)(2,1)S(1)}, bf16[1,192,768]{2,1,0:T(8,128)(2,1)S(1)}, u32[]{:S(2)}, u32[]{:S(2)}) collective-permute-start(bf16[1,192,768]{2,1,0:T(8,128)(2,1)S(1)} %constant_dynamic-slice_fusion), channel_id=1, source_target_pairs={{0,2},{1,3},{2,0},{3,1},{4,6},{5,7},{6,4},{7,5},{8,10},{9,11},{10,... | collective-permute-start | bytes 884744 | tf_op jit(solution)/shard_map/ppermute | solution.py:853
  286.1 45.8 %copy-start.1 = (f32[96,768]{1,0:T(8,128)S(1)}, f32[96,768]{1,0:T(8,128)}, u32[]{:S(2)}) copy-start(f32[96,768]{1,0:T(8,128)} %param.17) | copy-start | bytes 884740
  286.1 45.8 %copy-start.5 = (f32[96,768]{1,0:T(8,128)S(1)}, f32[96,768]{1,0:T(8,128)}, u32[]{:S(2)}) copy-start(f32[96,768]{1,0:T(8,128)} %param.18) | copy-start | bytes 884740
  286.1 45.8 %copy-start.6 = (f32[96,768]{1,0:T(8,128)S(1)}, f32[96,768]{1,0:T(8,128)}, u32[]{:S(2)}) copy-start(f32[96,768]{1,0:T(8,128)} %param.19) | copy-start | bytes 884740
  286.2 47.9 %copy-start.7 = (f32[13,24]{1,0:T(8,128)S(1)}, f32[13,24]{1,0:T(8,128)}, u32[]{:S(2)}) copy-start(f32[13,24]{1,0:T(8,128)} %param.23) | copy-start | bytes 3748
  286.2 47.9 %copy-start.8 = (f32[13,24]{1,0:T(8,128)S(1)}, f32[13,24]{1,0:T(8,128)}, u32[]{:S(2)}) copy-start(f32[13,24]{1,0:T(8,128)} %param.24) | copy-start | bytes 3748
  286.2 47.9 %copy-start.9 = (f32[13,24]{1,0:T(8,128)S(1)}, f32[13,24]{1,0:T(8,128)}, u32[]{:S(2)}) copy-start(f32[13,24]{1,0:T(8,128)} %param.25) | copy-start | bytes 3748

commit v3 on v2

--- a/solution.py
+++ b/solution.py
@@ -281,9 +281,9 @@
     pl.semaphore_wait(barrier, len(peers))
 
 
-def gathering_k1_body(wide, narrow, cols, steps, tok_ref, seg_ref, feat_ref, att_ref, ff_ref, vs_ref,
+def gathering_k1_body(wide, narrow, cols, steps, tok_ref, seg_ref, feat_ref, att_master, ff_master, vec_master,
                       mixed_ref, q_ref, k_ref, v_ref, ctx_ref, lse_ref, vec_ref, wout_ref, fout_ref,
-                      bias_scr, w_ref, vs_scr, put_sem, *sems):
+                      bias_scr, w_ref, vs_scr, att_ref, ff_ref, vs_ref, put_sem, *sems):
     i = pl.program_id(0)
     half = D // 2
     count = len(sems) // 3
@@ -296,13 +296,18 @@
 
     @pl.when(i == 0)
     def _():
+        att_ref[...] = att_master[...].astype(BF16)
+        ff_ref[...] = ff_master[...].astype(BF16)
+        vs_ref[...] = jnp.zeros_like(vs_ref)
+        vs_ref[0:vec_master.shape[0], 0:cols] = vec_master[...].astype(BF16)
         greet(wide, narrow)
         for one in (vs, att, ff):
             one.open()
         for k in range(narrow):
             vs.roots(k)
             att.roots(k)
-        ff.roots(0)
+            if k == 0:
+                ff.roots(0)
         for r in range(1, wide // 2):
             for k in range(narrow):
                 vs.relay(r, k)
@@ -349,23 +354,23 @@
 def gathering_k1(wide, narrow, tokens, seg, feat, att_shard, ff_shard, vec_shard):
     seqs, length = seg.shape
     n, devices = seqs * length, wide * narrow
-    vs = jnp.pad(vec_shard, ((0, 16 - vec_shard.shape[0]), (0, 128 - vec_shard.shape[1])))
     blk = pl.BlockSpec((length, D), lambda i: (i, 0))
     any_spec = pl.BlockSpec(memory_space=pl.ANY)
     o = lambda dt: jax.ShapeDtypeStruct((n, D), dt)
     sems = spreading_sems(wide, narrow, 2) * 2 + spreading_sems(wide, narrow, 1)
     return pl.pallas_call(
         partial(gathering_k1_body, wide, narrow, vec_shard.shape[1], seqs), grid=(seqs,),
-        in_specs=[blk, whole(seg.shape), whole(feat.shape), any_spec, any_spec, any_spec],
+        in_specs=[blk] + [whole(a.shape) for a in (seg, feat, att_shard, ff_shard, vec_shard)],
         out_specs=[blk] * 4 + [pl.BlockSpec((2, length, D), lambda i: (0, i, 0)), pl.BlockSpec((length, 128), lambda i: (i, 0)),
                                whole((16, D)), any_spec, any_spec],
         out_shape=[o(F32), o(BF16), o(BF16), o(BF16), jax.ShapeDtypeStruct((2, n, D), BF16), jax.ShapeDtypeStruct((n, 128), F32),
                    jax.ShapeDtypeStruct((16, D), F32), jax.ShapeDtypeStruct((4 * D, D), BF16), jax.ShapeDtypeStruct((2 * FF, D), BF16)],
-        scratch_shapes=[VMEM((length, length), F32), VMEM((4 * D, D), BF16), VMEM((16 * devices, 128), BF16), pltpu.SemaphoreType.DMA, *sems],
+        scratch_shapes=[VMEM((length, length), F32), VMEM((4 * D, D), BF16), VMEM((16 * devices, 128), BF16),
+                        VMEM(att_shard.shape, BF16), VMEM(ff_shard.shape, BF16), VMEM((16, 128), BF16), pltpu.SemaphoreType.DMA, *sems],
         compiler_params=pltpu.CompilerParams(collective_id=0, has_side_effects=True),
         cost_estimate=cost(60, 60),
         name="gather_attend",
-    )(tokens, seg, feat, att_shard, ff_shard, vs)
+    )(tokens, seg, feat, att_shard, ff_shard, vec_shard)
 
 def masks_of(bits):
     found = [0]
@@ -383,9 +388,11 @@
         self.rows = total.shape[1] // narrow
         self.orders = [bits, bits[::-1]]
         self.line_bits = [1 << b for b in range(narrow.bit_length() - 1)]
-        self.names = [("tree", h, t, m) for t in range(len(bits)) for h in range(2) for m in masks_of(self.orders[h][t + 1:])]
-        if line_refs:
-            self.names += [("line", 0, t, m) for t in range(len(self.line_bits)) for m in masks_of(self.line_bits[t + 1:])]
+        self.final = len(bits) - 1
+        self.blocks = sorted(range(narrow), key=lambda k: (1 - k % 2, k))
+        self.names = [("tree", h, t, m) for t in range(self.final) for h in range(2) for m in masks_of(self.orders[h][t + 1:])]
+        self.names += [("last", h, self.final, k) for k in self.blocks for h in range(2)]
+        self.names += [("line", 0, t, m) for t in range(len(line_refs)) for m in masks_of(self.line_bits[t + 1:])]
 
     def copy(self, name):
         kind, h, t, m = name
@@ -397,6 +404,12 @@
             source = self.total.at[flips(self.o, bit | m), :, cols]
             landing = self.tree_refs[t].at[h, slot]
             device = (2 * flips(self.o, bit) + self.c, self.z)
+        elif kind == "last":
+            bit = self.orders[h][t]
+            at, cols = self.block(m), pl.ds(h * (D // 2), D // 2)
+            source = self.total.at[flips(self.o, bit), at, cols]
+            landing = self.tree_refs[t].at[h, 0, at, :]
+            device = (2 * flips(self.o, bit) + self.c, self.z)
         else:
             bit = self.line_bits[t]
             slot = masks_of(self.line_bits[t + 1:]).index(m)
@@ -405,10 +418,26 @@
             device = (2 * self.o + self.c, flips(self.z, bit))
         return pltpu.make_async_remote_copy(source, landing, self.sems[0].at[n], self.sems[1].at[n], device_id=device, device_id_type=MESH)
 
+    def block(self, k):
+        return pl.ds(pl.multiple_of(flips(self.z, k) * self.rows, 8), self.rows)
+
+    def take_last(self, onward):
+        for name in self.names:
+            if name[0] == "last" and (name[3] % 2 == 1) == onward:
+                self.copy(name).wait_recv()
+                _, h, t, k = name
+                at, cols = self.block(k), pl.ds(h * (D // 2), D // 2)
+                self.total[self.o, at, cols] = self.total[self.o, at, cols] + self.tree_refs[t][h, 0, at, :]
+
     def pick(self, kind, turn, deep):
         return [n for n in self.names if n[0] == kind and n[2] == turn and (n[3] != 0) == deep]
 
     def send(self, kind, turn):
+        if kind == "tree" and turn == self.final:
+            for name in self.names:
+                if name[0] == "last":
+                    self.copy(name).start()
+            return
         for deep in (True, False):
             for name in self.pick(kind, turn, deep):
                 self.copy(name).start()
@@ -431,15 +460,14 @@
             self.copy(name).wait_send()
 
 
-def halving_scratch(wide, narrow, rows, line):
+def halving_scratch(wide, narrow, rows, left):
     outer, inner = (wide // 2).bit_length() - 1, narrow.bit_length() - 1
     groups = wide // 2
     shapes = [VMEM((groups, narrow * rows, D), BF16)]
     shapes += [VMEM((2, groups >> (t + 1), narrow * rows, D // 2), BF16) for t in range(outer)]
-    count = 2 * (groups - 1)
-    if line:
-        shapes += [VMEM((narrow >> (t + 1), rows, D), BF16) for t in range(inner)]
-        count += narrow - 1
+    count = 2 * (groups - 2) + 2 * narrow
+    shapes += [VMEM((narrow >> (t + 1), rows, D), BF16) for t in range(inner - left)]
+    count += sum(narrow >> (t + 1) for t in range(inner - left))
     return shapes + [pltpu.SemaphoreType.DMA((count,)), pltpu.SemaphoreType.DMA((count,))]
 
 
@@ -637,20 +665,21 @@
 def summing_k3_body(wide, narrow, steps, *refs):
     ins, (mine_ref, got_ref, d_ref, vg_ref, own_ref), rest = refs[:8], refs[8:13], refs[13:]
     (bias_scr, lse_scr, del_scr, total), rest = rest[:4], rest[4:]
-    *tree_refs, out_sems, in_sems = rest
+    *land_refs, out_sems, in_sems = rest
     i = pl.program_id(0)
-    turns = len(tree_refs)
-    half = Halving(wide, narrow, total, tree_refs, [], (out_sems, in_sems))
+    turns = (wide // 2).bit_length() - 1
+    tree_refs, line_refs = land_refs[:turns], land_refs[turns:]
+    half = Halving(wide, narrow, total, tree_refs, line_refs, (out_sems, in_sems))
 
     @pl.when(i == 0)
     def _():
-        greet(wide, 1)
+        greet(wide, narrow)
         begin_total(total, mine_ref, got_ref)
         half.send("tree", 0)
 
     def service(point):
         for t in range(turns):
-            spot = 3 * steps * (t + 1) // (turns + 1) - 1 if t < turns - 1 else 3 * steps - 2
+            spot = 3 * steps * (t + 1) // (turns + 1) - 1 if t < turns - 1 else 3 * steps - 4
             if spot % 3 == point:
                 @pl.when(i == spot // 3)
                 def _(t=t):
@@ -660,13 +689,24 @@
                     else:
                         for done in range(turns):
                             half.take("tree", done, False)
+                        half.take_last(True)
+                        if line_refs:
+                            half.send("line", 0)
 
     attend_back_step(i, *ins, d_ref, vg_ref, bias_scr, lse_scr, del_scr, service)
 
     @pl.when(i == steps - 1)
     def _():
+        half.take_last(False)
+        for t in range(len(line_refs)):
+            half.take("line", t, True)
+            half.take("line", t, False)
+            if t + 1 < len(line_refs):
+                half.send("line", t + 1)
         half.drain()
-        own_ref[...] = total[lax.axis_index("wide") // 2]
+        far = narrow // 2
+        for n, mask in enumerate((0, far) if far else (0,)):
+            own_ref[n] = total[half.o, pl.ds(pl.multiple_of(flips(half.z, mask) * half.rows, 8), half.rows), :]
 
 
 def summing_k3(wide, narrow, q, k, v, ctx, dctx, fb, lse, seg, mine, got):
@@ -678,10 +718,10 @@
         partial(summing_k3_body, wide, narrow, seqs), grid=(seqs,),
         in_specs=[blk] * 3 + [pl.BlockSpec((1, length, D), lambda i: (1, i, 0)), blk, blk,
                               pl.BlockSpec((length, 128), lambda i: (i, 0)), whole((seqs, length)), whole(mine.shape), whole(got.shape)],
-        out_specs=[pl.BlockSpec((4, length, D), lambda i: (0, i, 0)), whole((8, D)), whole((span, D))],
-        out_shape=[jax.ShapeDtypeStruct((4, n, D), BF16), jax.ShapeDtypeStruct((8, D), F32), jax.ShapeDtypeStruct((span, D), BF16)],
+        out_specs=[pl.BlockSpec((4, length, D), lambda i: (0, i, 0)), whole((8, D)), whole((2, span // narrow, D))],
+        out_shape=[jax.ShapeDtypeStruct((4, n, D), BF16), jax.ShapeDtypeStruct((8, D), F32), jax.ShapeDtypeStruct((2, span // narrow, D), BF16)],
         scratch_shapes=[VMEM((length, length), F32), VMEM((16, length), F32), VMEM((16, length), F32),
-                        *halving_scratch(wide, narrow, span // narrow, False)],
+                        *halving_scratch(wide, narrow, span // narrow, 1)],
         compiler_params=pltpu.CompilerParams(collective_id=1, has_side_effects=True),
         cost_estimate=cost(60, 40),
         name="attend_back_sum",
@@ -721,11 +761,14 @@
     half = Halving(wide, narrow, total, tree_refs, line_refs, (out_sems, in_sems))
     w, z = lax.axis_index("wide"), lax.axis_index("narrow")
     o, c = w // 2, w % 2
-    peers = [(2 * o + 1 - c, z)] + [(2 * flips(o, 1 << b) + c, z) for b in range(outer)] + [(w, flips(z, 1 << b)) for b in range(inner)]
-
-    def across(n):
-        return pltpu.make_async_remote_copy(sum_scr.at[n], came_scr.at[n], vec_sems_out.at[n], vec_sems_in.at[n],
-                                            device_id=peers[n], device_id_type=MESH)
+    ones = [(2 * o + 1 - c, z)] + [(2 * flips(o, 1 << b) + c, z) for b in range(outer)]
+    line = [(w, flips(z, k)) for k in range(1, narrow)]
+
+    def across(n, peer):
+        return pltpu.make_async_remote_copy(sum_scr.at[min(n, len(ones))], came_scr.at[n], vec_sems_out.at[n], vec_sems_in.at[n],
+                                            device_id=peer, device_id_type=MESH)
+
+    hops = [across(n, peer) for n, peer in enumerate(ones + line)]
 
     @pl.when(i == 0)
     def _():
@@ -733,10 +776,17 @@
         begin_total(total, mine_ref, got_ref)
         half.send("tree", 0)
 
+    @pl.when(i == steps - 1)
+    def _():
+        for t in range(outer):
+            half.take("tree", t, False)
+        half.take_last(True)
+        half.send("line", 0)
+
     token_back_step(i, *ins, tg_ref, vg_scr)
 
     for t in range(outer - 1):
-        @pl.when(i == min(steps - 1, (steps * (t + 1)) // (outer + 1)))
+        @pl.when(i == min(steps - 2, (steps * (t + 1)) // (outer + 1)))
         def _(t=t):
             half.take("tree", t, True)
             half.send("tree", t + 1)
@@ -747,36 +797,29 @@
         sum_scr[0, 1:3, :] = vg3_ref[0:2, :]
         sum_scr[0, 3:13, :] = vg2_ref[0:10, :]
         sum_scr[0, 13:16, :] = jnp.zeros((3, D), F32)
-        across(0).start()
-        for t in range(outer):
-            half.take("tree", t, False)
-        half.send("line", 0)
-        turn = 0
-        for n in range(len(peers)):
-            across(n).wait_recv()
-            added = sum_scr[n] + came_scr[n]
-            if n + 1 < len(peers):
-                sum_scr[n + 1] = added
-                across(n + 1).start()
-            else:
-                vec_out[...] = added
-            if n % 2 == 1 and turn < inner - 1:
-                half.take("line", turn, True)
-                half.take("line", turn, False)
-                turn += 1
-                half.send("line", turn)
-        while turn < inner - 1:
+        hops[0].start()
+        half.take_last(False)
+        for turn in range(inner - 1):
             half.take("line", turn, True)
             half.take("line", turn, False)
-            turn += 1
-            half.send("line", turn)
+            half.send("line", turn + 1)
+        for n in range(len(ones)):
+            hops[n].wait_recv()
+            sum_scr[n + 1] = sum_scr[n] + came_scr[n]
+            for later in (hops[n + 1:n + 2] if n + 1 < len(ones) else hops[n + 1:]):
+                later.start()
+        for hop in hops[len(ones):]:
+            hop.wait_recv()
+        spots = [sum_scr[len(ones)]] + [came_scr[len(ones) + k] for k in range(narrow - 1)]
+        vec_out[...] = sum(spots[1:], spots[0])
+        turn = inner - 1
         last = half.pick("line", turn, False)[0]
         half.copy(last).wait_recv()
         at = pl.ds(pl.multiple_of(z * half.rows, 8), half.rows)
         own_ref[...] = total[o, at, :].astype(F32) + line_refs[turn][0].astype(F32)
         half.drain()
-        for n in range(len(peers)):
-            across(n).wait_send()
+        for hop in hops:
+            hop.wait_send()
 
 
 def summing_k4(wide, narrow, first, d, tokens, seg, feat, att, vec, mine, got, vg2, vg3):
@@ -784,7 +827,7 @@
     n = seqs * length
     blk = pl.BlockSpec((length, D), lambda i: (i, 0))
     rows = mine.shape[1] // narrow
-    stages = (wide * narrow).bit_length() - 1
+    stages = (wide // 2).bit_length() + narrow - 1
     return pl.pallas_call(
         partial(summing_k4_body, wide, narrow, seqs), grid=(seqs,),
         in_specs=[blk, pl.BlockSpec((3, length, D), lambda i: (0, i, 0)), blk, whole(seg.shape), whole(feat.shape),
@@ -792,7 +835,7 @@
                   whole(mine.shape), whole(got.shape), whole(vg2.shape), whole(vg3.shape)],
         out_specs=[blk, whole((rows, D)), whole((16, D))],
         out_shape=[jax.ShapeDtypeStruct((n, D), BF16), jax.ShapeDtypeStruct((rows, D), F32), jax.ShapeDtypeStruct((16, D), F32)],
-        scratch_shapes=[VMEM((8, D), F32), *halving_scratch(wide, narrow, rows, True),
+        scratch_shapes=[VMEM((8, D), F32), *halving_scratch(wide, narrow, rows, 0),
                         VMEM((stages, 16, D), F32), VMEM((stages, 16, D), F32), pltpu.SemaphoreType.DMA((stages,)), pltpu.SemaphoreType.DMA((stages,))],
         compiler_params=pltpu.CompilerParams(collective_id=2, has_side_effects=True),
         cost_estimate=cost(30, 30),
@@ -913,11 +956,6 @@
         total = add(mine, got)
         width = len(self.orders[0])
         self.values = [h.reshape((2,) * width + h.shape[1:]) for h in (total[:, :, :D // 2], total[:, :, D // 2:])]
-        self.split()
-
-    def resume(self, own):
-        self.done = len(self.orders[0])
-        self.values = [own]
         self.split()
 
     def split(self):
@@ -1089,12 +1127,12 @@
     me1 = me.reshape(1).astype(jnp.int32)
     seg, feat = segment_ids, feature_ids
     seqs = seg.shape[0]
-    shards = [m.astype(BF16) for m in (attention_master, feedforward_master, vector_master)]
+    shards = (attention_master, feedforward_master, vector_master)
     if devices <= 32:
         *held, vec, natural, ff = gathering_k1(wide, narrow, tokens, seg, feat, *shards)
         ff, offsets = [ff], ()
     else:
-        *held, vec, natural, ff, offsets = forward_by_permutes(me, wide, narrow, tokens, seg, feat, *shards)
+        *held, vec, natural, ff, offsets = forward_by_permutes(me, wide, narrow, tokens, seg, feat, *[m.astype(BF16) for m in shards])
     mixed, q, k, v, ctx, lse = held
     out, first, fb, dctx, broad, slim, vg2 = k2(me1, mixed, ctx, cotangent, natural, ff, offsets, vec)
     parts = (first, fb, dctx, broad, slim, vg2)
@@ -1102,17 +1140,13 @@
     if devices <= 32:
         mine, got = split_grads(me, broad, slim, wide, narrow, rows[0])
         d, vg3, own = summing_k3(wide, narrow, q, k, v, ctx, dctx, fb, lse, seg, mine, got)
-        ff_sum = Scatter(me, wide, narrow)
-        ff_sum.resume(own)
-        lhs, ff_owned = ctx, None
-        sent, ff_owned = ff_sum.over((lhs, d), lambda g: one_side(me, *g, wide, narrow, rows[1], False))
+        own, away, lhs = tie(own[0], own[1], ctx)
+        came = swap(away, narrow // 2, devices)
+        sent = one_side(me, lhs, d, wide, narrow, rows[1], False)
+        came, sent, lhs = tie(came, sent, lhs)
         back = swap(sent, narrow, devices)
-        if ff_owned is None:
-            mine, ff_owned = ff_sum.over((lhs, d), lambda g: one_side(me, *g, wide, narrow, rows[1], True))
-        else:
-            mine = one_side(me, lhs, d, wide, narrow, rows[1], True)
-        while ff_owned is None:
-            _, ff_owned = ff_sum.over((), lambda g: ())
+        mine = one_side(me, lhs, d, wide, narrow, rows[1], True)
+        ff_owned = add(own, came, F32)
         token_grads, att_owned, vec_sum = summing_k4(wide, narrow, first, d, tokens, seg, feat, natural, vec, mine, back, vg2, vg3)
         width = vector_master.shape[1]
         vec_owned = lax.dynamic_slice(vec_sum, (0, me * width), (vector_master.shape[0], width))

time: 340 us -> 327 us (0.962)
  waiting for transfers between devices: 8.37 us -> 1.17 us
  other arithmetic: 9.51 us -> 5.21 us
    ppermute x4 -> x3, waiting for transfers between devices: 8.37 us -> 1.17 us  [swap(): return lax.ppermute(value, BOTH, [(i, i ^ bit) for i in range(devices)])]
    convert_element_type x4 -> x0, other arithmetic: 4.3 us -> none  [the longest x3 4.15 us: local(): m.astype(BF16)]
    pallas_call x1, Pallas kernels: 92.2 us -> 88.8 us  [gathering_k1(): pl.pallas_call(partial(gathering_k1_body, wide, narrow, vec_shard.shape[1...]
  transfers between devices with their start and end apart: 4 -> 3, of which waited for: 2 -> 1; matrix products, arithmetic and copies ran while one was open for 1% -> 1% of each run, Pallas kernels for 11% -> 11%
where the time goes in v3:
time: 327 us
  Pallas kernels  312 us (95%)
  other arithmetic  5.21 us (2%)
  local copies, waits for them, and re-layouts  4.89 us (1%)
    pallas_call x1, Pallas kernels, gathering_k1(): pl.pallas_call(partial(gathering_k1_body, wide, narrow, vec_shard.shape[1...  88.8 us
    pallas_call x1, Pallas kernels, k2(): pl.pallas_call(partial(k2_body, offsets), grid_spec=pltpu.PrefetchScalarG...  68.2 us
    pallas_call x1, Pallas kernels, summing_k3(): pl.pallas_call(partial(summing_k3_body, wide, narrow, seqs), grid=(seqs,)...  59.1 us
    pallas_call x4, Pallas kernels, dw(): pl.pallas_call(partial(dw_body, rows), grid_spec=pltpu.PrefetchScalarGrid...  50.9 us
    pallas_call x1, Pallas kernels, summing_k4(): pl.pallas_call(partial(summing_k4_body, wide, narrow, seqs), grid=(seqs,)...  45.1 us
  transfers between devices with their start and end apart: 3, of which 1 were waited for; matrix products, arithmetic and copies ran while one was open for 1% of the time, Pallas kernels for 11%

profile of v3, /device:TPU:0, one launch (start us, length us, event | category | flops | bytes accessed | tf_op | source)
XLA Modules:
  0.0 327.0 jit_solution(1595416407540947288)
XLA Ops:
  0.7 88.8 %gather_attend.1 = (f32[2048,768]{1,0:T(8,128)}, bf16[2048,768]{1,0:T(8,128)(2,1)}, bf16[2048,768]{1,0:T(8,128)(2,1)}, bf16[2048,768]{1,0:T(8,128)(2,1)}, bf16[2...) custom-call(bf16[2048,768]{1,0:T(8,128)(2,1)} %refs_2_.1, ...), custom_call_target="tpu_custom_call" | custom-call | flops 60000002048 | bytes 60000000 | tf_op jit(solution)/shard_map/gather_attend/pallas_call | solution.py:361
  89.4 68.2 %feed_forward.1 = (bf16[2048,768]{1,0:T(8,128)(2,1)}, f32[2048,768]{1,0:T(8,128)}, bf16[2048,768]{1,0:T(8,128)(2,1)}, bf16[2048,768]{1,0:T(8,128)(2,1)}, bf16[2,...) custom-call(s32[1]{0:T(128)} %bitcast.self_ref, ...), custom_call_target="tpu_custom_call" | custom-call | flops 60000002048 | bytes 80000000 | tf_op jit(solution)/shard_map/feed_forward/pallas_call | solution.py:553
  157.6 15.1 %weight_grad.4 = bf16[4,768,768]{2,1,0:T(8,128)(2,1)} custom-call(s32[1]{0:T(128)} %bitcast.2.side_ref, bf16[2,2048,3072]{2,1,0:T(8,128)(2,1)} %get-tuple-element.59.lhs_ref, bf16[2,2048,768]{2,1,0:T(8,128)(2,1)} %get-tuple-element.58.rhs_ref), custom_call_target="tpu_custom_call" | custom-call | flops 9663676416 | bytes 10000000 | tf_op jit(solution)/shard_map/weight_grad/pallas_call | solution.py:582
  172.7 0.5 collective-permute-start
  173.2 15.1 %weight_grad.5.refs_8_ = bf16[4,768,768]{2,1,0:T(8,128)(2,1)} custom-call(s32[1]{0:T(128)} %bitcast.1.side_ref, bf16[2,2048,3072]{2,1,0:T(8,128)(2,1)} %get-tuple-element.59.lhs_ref, bf16[2,2048,768]{2,1,0:T(8,128)(2,1)} %get-tuple-element.58.rhs_ref), custom_call_target="tpu_custom_call" | custom-call | flops 9663676416 | bytes 10000000 | tf_op jit(solution)/shard_map/weight_grad/pallas_call | solution.py:582
  188.3 0.0 collective-permute-done.refs_9_
  188.3 59.1 %attend_back_sum.1 = (bf16[4,2048,768]{2,1,0:T(8,128)(2,1)}, f32[8,768]{1,0:T(8,128)}, bf16[2,192,768]{2,1,0:T(8,128)(2,1)}) custom-call(bf16[2048,768]{1,0:T(8,128)(2,1)} %get-tuple-element.51.refs_0_, bf16[2048,768]{1,0:T(8,128)(2,1)} %get-tuple-element.52.refs_1_, bf16[2048,768]{1,0:T(8,128)(2,1)} %get-tuple-element.53.refs_2_, ...), custom_call_target="tpu_custom_call" | custom-call | flops 60000002048 | bytes 40000000 | tf_op jit(solution)/shard_map/attend_back_sum/pallas_call | solution.py:717
  247.4 1.1 slice_bitcast_fusion
  248.4 2.4 collective-permute-start.1
  250.9 10.4 %weight_grad.6 = bf16[4,384,768]{2,1,0:T(8,128)(2,1)} custom-call(s32[1]{0:T(128)} %bitcast.2.side_ref, bf16[2,2048,768]{2,1,0:T(8,128)(2,1)} %get-tuple-element.65.ctx_ref.refs_3_.lhs_ref, bf16[4,2048,768]{2,1,0:T(8,128)(2,1)} %get-tuple-element.61.rhs_ref.refs_1_), custom_call_target="tpu_custom_call" | custom-call | flops 4831838208 | bytes 10000000 | tf_op jit(solution)/shard_map/weight_grad/pallas_call | solution.py:582
  261.3 1.2 collective-permute-done.1
  262.5 0.0 collective-permute-start.2
  262.5 1.7 fusion.5
  264.2 10.3 %weight_grad.7.refs_7_ = bf16[4,384,768]{2,1,0:T(8,128)(2,1)} custom-call(s32[1]{0:T(128)} %bitcast.1.side_ref, bf16[2,2048,768]{2,1,0:T(8,128)(2,1)} %get-tuple-element.65.ctx_ref.refs_3_.lhs_ref, bf16[4,2048,768]{2,1,0:T(8,128)(2,1)} %get-tuple-element.61.rhs_ref.refs_1_), custom_call_target="tpu_custom_call" | custom-call | flops 4831838208 | bytes 10000000 | tf_op jit(solution)/shard_map/weight_grad/pallas_call | solution.py:582
  274.5 0.0 collective-permute-done.2.refs_8_
  274.5 0.0 copy-start.5
  274.5 0.0 copy-start.6
  274.5 0.0 copy-start.7
  274.6 0.0 copy-start.8
  274.6 45.1 %token_grad_sum.1 = (bf16[2048,768]{1,0:T(8,128)(2,1)}, f32[96,768]{1,0:T(8,128)}, f32[16,768]{1,0:T(8,128)}) custom-call(f32[2048,768]{1,0:T(8,128)} %get-tuple-element.50.refs_0_, bf16[4,2048,768]{2,1,0:T(8,128)(2,1)} %get-tuple-element.61.rhs_ref.refs_1_, bf16[2048,768]{1,0:T(8,128)(2,1)} %refs_2_.1, s32[4,512]{1,0:T(4,128)} %refs_3_.1, ...), custom_call_target="tpu_custom_call" | custom-call | flops 30000001024 | bytes 30000000 | tf_op jit(solution)/shard_map/token_grad_sum/pallas_call | solution.py:831
  319.7 2.1 fusion.7
  321.8 0.0 copy-done.7
  321.8 1.4 fusion.3
  323.2 3.8 %copy.28 = bf16[2048,768]{1,0:T(8,128)(2,1)} copy(bf16[2048,768]{1,0:T(8,128)(2,1)} %get-tuple-element.103) | data formatting | bytes 6291456
  (15 shorter events, 0.0 us)
Async XLA Ops:
  172.7 15.6 %collective-permute-start = (bf16[4,768,768]{2,1,0:T(8,128)(2,1)}, bf16[4,768,768]{2,1,0:T(8,128)(2,1)}, u32[]{:S(2)}, u32[]{:S(2)}) collective-permute-start(bf16[4,768,768]{2,1,0:T(8,128)(2,1)} %weight_grad.4), channel_id=1, source_target_pairs={{0,4},{1,5},{2,6},{3,7},{4,0},{5,1},{6,2},{7,3},{8,12},{9,13},{10,... | collective-permute-start | bytes 14155784 | tf_op jit(solution)/shard_map/ppermute | solution.py:896
  248.4 14.0 %collective-permute-start.1 = (bf16[192,768]{1,0:T(8,128)(2,1)S(1)}, bf16[192,768]{1,0:T(8,128)(2,1)S(1)}, u32[]{:S(2)}, u32[]{:S(2)}) collective-permute-start(bf16[192,768]{1,0:T(8,128)(2,1)S(1)} %get-tuple-element.63), channel_id=1, source_target_pairs={{0,2},{1,3},{2,0},{3,1},{4,6},{5,7},{6,4},{7,5},{8,10},{9,11},{10,... | collective-permute-start | bytes 884744 | tf_op jit(solution)/shard_map/ppermute | solution.py:896
  250.9 11.6 %copy-start = (f32[192,768]{1,0:T(8,128)S(1)}, f32[192,768]{1,0:T(8,128)}, u32[]{:S(2)}) copy-start(f32[192,768]{1,0:T(8,128)} %ff_master.1) | copy-start | bytes 1769476
  250.9 11.6 %copy-start.1 = (f32[192,768]{1,0:T(8,128)S(1)}, f32[192,768]{1,0:T(8,128)}, u32[]{:S(2)}) copy-start(f32[192,768]{1,0:T(8,128)} %param.21) | copy-start | bytes 1769476
  250.9 11.6 %copy-start.2 = (f32[192,768]{1,0:T(8,128)S(1)}, f32[192,768]{1,0:T(8,128)}, u32[]{:S(2)}) copy-start(f32[192,768]{1,0:T(8,128)} %param.22) | copy-start | bytes 1769476
  262.5 12.0 %collective-permute-start.2 = (bf16[4,384,768]{2,1,0:T(8,128)(2,1)}, bf16[4,384,768]{2,1,0:T(8,128)(2,1)}, u32[]{:S(2)}, u32[]{:S(2)}) collective-permute-start(bf16[4,384,768]{2,1,0:T(8,128)(2,1)} %weight_grad.6), channel_id=1, source_target_pairs={{0,4},{1,5},{2,6},{3,7},{4,0},{5,1},{6,2},{7,3},{8,12},{9,13},{10,... | collective-permute-start | bytes 7077896 | tf_op jit(solution)/shard_map/ppermute | solution.py:896
  274.5 45.2 %copy-start.3 = (f32[96,768]{1,0:T(8,128)S(1)}, f32[96,768]{1,0:T(8,128)}, u32[]{:S(2)}) copy-start(f32[96,768]{1,0:T(8,128)} %att_master.1) | copy-start | bytes 884740
  274.5 45.2 %copy-start.4 = (f32[96,768]{1,0:T(8,128)S(1)}, f32[96,768]{1,0:T(8,128)}, u32[]{:S(2)}) copy-start(f32[96,768]{1,0:T(8,128)} %param.18) | copy-start | bytes 884740
  274.5 45.2 %copy-start.5 = (f32[96,768]{1,0:T(8,128)S(1)}, f32[96,768]{1,0:T(8,128)}, u32[]{:S(2)}) copy-start(f32[96,768]{1,0:T(8,128)} %param.19) | copy-start | bytes 884740
  274.5 47.2 %copy-start.6 = (f32[13,24]{1,0:T(8,128)S(1)}, f32[13,24]{1,0:T(8,128)}, u32[]{:S(2)}) copy-start(f32[13,24]{1,0:T(8,128)} %vec_master.1) | copy-start | bytes 3748
  274.5 47.2 %copy-start.7 = (f32[13,24]{1,0:T(8,128)S(1)}, f32[13,24]{1,0:T(8,128)}, u32[]{:S(2)}) copy-start(f32[13,24]{1,0:T(8,128)} %param.24) | copy-start | bytes 3748
  274.6 47.2 %copy-start.8 = (f32[13,24]{1,0:T(8,128)S(1)}, f32[13,24]{1,0:T(8,128)}, u32[]{:S(2)}) copy-start(f32[13,24]{1,0:T(8,128)} %param.25) | copy-start | bytes 3748
